TPU v7x, 32 devices: a whole 2x2x4 slice. The times are simulated.
32 devices in a mesh: dp: 8 (over z, core), seq: 4 (over y, x).
Axes of the slice: x: 2, y: 2, z: 4, core: 2. Of those that a mesh axis runs over, the one named last changes fastest.
Arguments:
- tokens: bfloat16 [2, 8, 512, 768], P(None, 'dp', 'seq'), may hold values from -6 to 6
- piece_starts: int32 [2, 8, 2], P(None, 'dp'), may hold values from 0 to 256, as said below
- qkv_weight: bfloat16 [768, 2304], P(('dp', 'seq')), may hold values from -0.21875 to 0.21875
- qv_bias: bfloat16 [1536], P(('dp', 'seq')), may hold values from -1.796875 to 1.796875
- out_weight: bfloat16 [768, 768], P(('dp', 'seq')), may hold values from -1.25 to 1.25
- out_bias: bfloat16 [768], P(('dp', 'seq')), may hold values from -1.796875 to 1.796875
- norm1_gain: bfloat16 [768], P(('dp', 'seq')), may hold values from 0.5 to 1.5
- norm1_bias: bfloat16 [768], P(('dp', 'seq')), may hold values from -1.796875 to 1.796875
- up_weight: bfloat16 [768, 3072], P(('dp', 'seq')), may hold values from -0.21875 to 0.21875
- up_bias: bfloat16 [3072], P(('dp', 'seq')), may hold values from -1.796875 to 1.796875
- down_weight: bfloat16 [3072, 768], P(('dp', 'seq')), may hold values from -0.109375 to 0.109375
- down_bias: bfloat16 [768], P(('dp', 'seq')), may hold values from -1.796875 to 1.796875
- norm2_gain: bfloat16 [768], P(('dp', 'seq')), may hold values from 0.5 to 1.5
- norm2_bias: bfloat16 [768], P(('dp', 'seq')), may hold values from -1.796875 to 1.796875
- grad_out: bfloat16 [2, 8, 512, 768], P(None, 'dp', 'seq'), may hold values from -6 to 6
Outputs:
- layer_out: bfloat16 [2, 8, 512, 768], P(None, 'dp', 'seq')
- tokens_grad: float32 [2, 8, 512, 768], P(None, 'dp', 'seq')
- qkv_weight_grad: float32 [768, 2304], P(('dp', 'seq'))
- qv_bias_grad: float32 [1536], P(('dp', 'seq'))
- out_weight_grad: float32 [768, 768], P(('dp', 'seq'))
- out_bias_grad: float32 [768], P(('dp', 'seq'))
- norm1_gain_grad: float32 [768], P(('dp', 'seq'))
- norm1_bias_grad: float32 [768], P(('dp', 'seq'))
- up_weight_grad: float32 [768, 3072], P(('dp', 'seq'))
- up_bias_grad: float32 [3072], P(('dp', 'seq'))
- down_weight_grad: float32 [3072, 768], P(('dp', 'seq'))
- down_bias_grad: float32 [768], P(('dp', 'seq'))
- norm2_gain_grad: float32 [768], P(('dp', 'seq'))
- norm2_bias_grad: float32 [768], P(('dp', 'seq'))
Inputs may be any that keep to these rules, and one draw needn't show every extreme that they name: `piece_starts`: each sequence's 2 pieces of 256 positions lie inside it, in rising order, without intersection.
All inputs are finite; a program needn't handle non-finite values.
Results may differ from a plain program's by a relative error of at most 0.018.
Values may be sent and summed in bfloat16 or wider, within the bound.
A program may use at most 192 MiB of HBM per device.

v0:
```python
import math

import jax
import jax.numpy as jnp
from jax import lax
from jax.sharding import PartitionSpec as P

HEADS = 12
PIC = 256


NEG = -1e30
EPS = 1e-05


def owners(positions, starts):
    inside = (positions[:, None] >= starts[None, :]) & (positions[:, None] < starts[None, :] + PIC)
    return jnp.max(jnp.where(inside, starts[None, :], -1), axis=1)


def visible_mask(query_pos, query_owner, key_pos, key_owner):
    later = key_pos[None, :] <= query_pos[:, None]
    shared = (key_owner[None, :] == query_owner[:, None]) & (query_owner[:, None] >= 0)
    return later | shared


def normalize(values):
    centre = values - jnp.mean(values, axis=-1, keepdims=True)
    inverse = lax.rsqrt(jnp.mean(centre * centre, axis=-1, keepdims=True) + EPS)
    return (centre * inverse, inverse)


def norm_back(upstream, normed, inverse, gain):
    scaled = upstream * gain
    return inverse * (
        scaled
        - jnp.mean(scaled, axis=-1, keepdims=True)
        - normed * jnp.mean(scaled * normed, axis=-1, keepdims=True)
    )


def matmul(left, right):
    return jnp.dot(left, right, preferred_element_type=jnp.float32)


def left_trans(left, right):
    return lax.dot_general(
        left, right, (((0,), (0,)), ((), ())), preferred_element_type=jnp.float32
    )


def right_trans(left, right):
    return lax.dot_general(
        left, right, (((1,), (1,)), ((), ())), preferred_element_type=jnp.float32
    )


def key_blocks(count):
    size = math.gcd(count, 1024)
    return (size, count // size)


def gather_forward(shards):
    return (
        lax.all_gather(shards[0], ("dp", "seq"), axis=0, tiled=True),
        lax.all_gather(shards[1], ("dp", "seq"), axis=0, tiled=True),
        lax.all_gather(shards[2], ("dp", "seq"), axis=0, tiled=True),
        lax.all_gather(shards[3], ("dp", "seq"), axis=0, tiled=True),
        lax.all_gather(shards[4], ("dp", "seq"), axis=0, tiled=True),
        lax.all_gather(shards[5], ("dp", "seq"), axis=0, tiled=True),
        lax.all_gather(shards[6], ("dp", "seq"), axis=0, tiled=True),
        lax.all_gather(shards[7], ("dp", "seq"), axis=0, tiled=True),
        lax.all_gather(shards[8], ("dp", "seq"), axis=0, tiled=True),
        lax.all_gather(shards[9], ("dp", "seq"), axis=0, tiled=True),
        lax.all_gather(shards[10], ("dp", "seq"), axis=0, tiled=True),
        lax.all_gather(shards[11], ("dp", "seq"), axis=0, tiled=True),
    )


def gather_backward(shards):
    return (
        lax.all_gather(shards[0], ("dp", "seq"), axis=0, tiled=True),
        lax.all_gather(shards[1], ("dp", "seq"), axis=0, tiled=True),
        lax.all_gather(shards[2], ("dp", "seq"), axis=0, tiled=True),
        lax.all_gather(shards[3], ("dp", "seq"), axis=0, tiled=True),
        lax.all_gather(shards[4], ("dp", "seq"), axis=0, tiled=True),
        lax.all_gather(shards[5], ("dp", "seq"), axis=0, tiled=True),
        lax.all_gather(shards[6], ("dp", "seq"), axis=0, tiled=True),
        lax.all_gather(shards[7], ("dp", "seq"), axis=0, tiled=True),
        lax.all_gather(shards[8], ("dp", "seq"), axis=0, tiled=True),
        lax.all_gather(shards[9], ("dp", "seq"), axis=0, tiled=True),
        lax.all_gather(shards[10], ("dp", "seq"), axis=0, tiled=True),
        lax.all_gather(shards[11], ("dp", "seq"), axis=0, tiled=True),
    )


def column_sum(values):
    return jnp.sum(values.astype(jnp.float32), axis=0)


def on_device(
    tokens,
    piece_starts,
    qkv_weight,
    qv_bias,
    out_weight,
    out_bias,
    norm1_gain,
    norm1_bias,
    up_weight,
    up_bias,
    down_weight,
    down_bias,
    norm2_gain,
    norm2_bias,
    grad_out,
):
    shards = (
        qkv_weight,
        qv_bias,
        out_weight,
        out_bias,
        norm1_gain,
        norm1_bias,
        up_weight,
        up_bias,
        down_weight,
        down_bias,
        norm2_gain,
        norm2_bias,
    )
    micro_count = tokens.shape[0]
    rows = tokens.shape[2]
    width = tokens.shape[3]
    head_size = width // HEADS
    scale = 1.0 / math.sqrt(head_size)
    length = rows * lax.axis_size("seq")
    query_pos = lax.axis_index("seq") * rows + jnp.arange(rows, dtype=jnp.int32)
    totals = None
    outputs = []
    input_grads = []
    for micro in range(micro_count):
        params = gather_forward(shards)
        (
            full_qkv,
            full_qvb,
            full_out,
            full_outb,
            full_g1,
            full_b1,
            full_up,
            full_upb,
            full_down,
            full_downb,
            full_g2,
            full_b2,
        ) = params
        starts = piece_starts[micro, 0]
        query_owner = owners(query_pos, starts)
        source = tokens[micro, 0]
        joined = matmul(source, full_qkv)
        queries = (joined[:, :width] + full_qvb[:width].astype(jnp.float32)).astype(jnp.bfloat16)
        keys = joined[:, width : 2 * width].astype(jnp.bfloat16)
        values = (joined[:, 2 * width :] + full_qvb[width:].astype(jnp.float32)).astype(
            jnp.bfloat16
        )
        query_heads = queries.reshape(rows, HEADS, head_size)

        def block_scores(key_block, key_pos):
            scores = (
                jnp.einsum(
                    "qhd,khd->hqk", query_heads, key_block, preferred_element_type=jnp.float32
                )
                * scale
            )
            allowed = visible_mask(query_pos, query_owner, key_pos, owners(key_pos, starts))
            return jnp.where(allowed[None], scores, NEG)

        initial = (
            jnp.full((HEADS, rows), NEG, jnp.float32),
            jnp.zeros((HEADS, rows), jnp.float32),
            jnp.zeros((HEADS, rows, head_size), jnp.float32),
        )
        key_piece = lax.all_gather(keys, "seq", axis=0, tiled=True)
        value_piece = lax.all_gather(values, "seq", axis=0, tiled=True)
        size, count = key_blocks(key_piece.shape[0])

        def one(block, carry):
            run_max, total, accum = carry
            key_block = lax.dynamic_slice_in_dim(key_piece, block * size, size, 0).reshape(
                size, HEADS, head_size
            )
            value_block = lax.dynamic_slice_in_dim(value_piece, block * size, size, 0).reshape(
                size, HEADS, head_size
            )
            key_pos = block * size + jnp.arange(size, dtype=jnp.int32)
            scores = block_scores(key_block, key_pos)
            new_max = jnp.maximum(run_max, jnp.max(scores, axis=-1))
            factor = jnp.exp(run_max - new_max)
            weights = jnp.exp(scores - new_max[:, :, None])
            total = total * factor + jnp.sum(weights, axis=-1)
            accum = accum * factor[:, :, None] + jnp.einsum(
                "hqk,khd->hqd",
                weights.astype(jnp.bfloat16),
                value_block,
                preferred_element_type=jnp.float32,
            )
            return (new_max, total, accum)

        run_max, total, accum = lax.fori_loop(0, count, one, initial)
        lse = run_max + jnp.log(total)
        exact = (accum / total[:, :, None]).transpose(1, 0, 2)
        attended = exact.reshape(rows, width).astype(jnp.bfloat16)
        resid1 = (
            source.astype(jnp.float32) + matmul(attended, full_out) + full_outb.astype(jnp.float32)
        )
        normed1, inverse1 = normalize(resid1)
        gain1 = full_g1.astype(jnp.float32)
        mixed1 = normed1 * gain1 + full_b1.astype(jnp.float32)
        inner = mixed1.astype(jnp.bfloat16)
        pre = matmul(inner, full_up) + full_upb.astype(jnp.float32)
        act = jax.nn.gelu(pre, approximate=False).astype(jnp.bfloat16)
        resid2 = mixed1 + matmul(act, full_down) + full_downb.astype(jnp.float32)
        normed2, inverse2 = normalize(resid2)
        gain2 = full_g2.astype(jnp.float32)
        outputs.append((normed2 * gain2 + full_b2.astype(jnp.float32)).astype(jnp.bfloat16))
        back = gather_backward(shards)
        back_qkv = back[0]
        back_out = back[2]
        back_up = back[6]
        back_down = back[8]
        cotan = grad_out[micro, 0].astype(jnp.float32)
        d_resid2 = norm_back(cotan, normed2, inverse2, gain2)
        grad_g2 = jnp.sum(cotan * normed2, axis=0)
        grad_b2 = jnp.sum(cotan, axis=0)
        d_branch2 = d_resid2.astype(jnp.bfloat16)
        grad_downb = column_sum(d_branch2)
        grad_down = left_trans(act, d_branch2)
        d_act = right_trans(d_branch2, back_down)
        gelu_value, gelu_back = jax.vjp(lambda value: jax.nn.gelu(value, approximate=False), pre)
        d_pre = gelu_back(d_act)[0].astype(jnp.bfloat16)
        grad_upb = column_sum(d_pre)
        grad_up = left_trans(inner, d_pre)
        d_mixed1 = d_resid2 + right_trans(d_pre, back_up)
        d_resid1 = norm_back(d_mixed1, normed1, inverse1, gain1)
        grad_g1 = jnp.sum(d_mixed1 * normed1, axis=0)
        grad_b1 = jnp.sum(d_mixed1, axis=0)
        d_branch1 = d_resid1.astype(jnp.bfloat16)
        grad_outb = column_sum(d_branch1)
        grad_out_w = left_trans(attended, d_branch1)
        d_attended = right_trans(d_branch1, back_out).astype(jnp.bfloat16)
        grad_heads = d_attended.reshape(rows, HEADS, head_size)
        delta = jnp.sum(grad_heads.astype(jnp.float32) * exact, axis=-1).T
        initial_back = (
            jnp.zeros((rows, HEADS, head_size), jnp.float32),
            jnp.zeros((length, width), jnp.float32),
            jnp.zeros((length, width), jnp.float32),
        )
        fold_key_piece = lax.all_gather(keys, "seq", axis=0, tiled=True)
        fold_value_piece = lax.all_gather(values, "seq", axis=0, tiled=True)
        fold_size, fold_count = key_blocks(fold_key_piece.shape[0])

        def fold_one(block, carry):
            query_grad, key_grads, value_grads = carry
            offset = block * fold_size
            key_block = lax.dynamic_slice_in_dim(fold_key_piece, offset, fold_size, 0).reshape(
                fold_size, HEADS, head_size
            )
            value_block = lax.dynamic_slice_in_dim(fold_value_piece, offset, fold_size, 0).reshape(
                fold_size, HEADS, head_size
            )
            key_pos = offset + jnp.arange(fold_size, dtype=jnp.int32)
            probs = jnp.exp(block_scores(key_block, key_pos) - lse[:, :, None])
            d_probs = jnp.einsum(
                "qhd,khd->hqk", grad_heads, value_block, preferred_element_type=jnp.float32
            )
            d_scores = (probs * (d_probs - delta[:, :, None])).astype(jnp.bfloat16)
            query_grad = (
                query_grad
                + jnp.einsum(
                    "hqk,khd->qhd", d_scores, key_block, preferred_element_type=jnp.float32
                )
                * scale
            )
            key_part = (
                jnp.einsum(
                    "hqk,qhd->khd", d_scores, query_heads, preferred_element_type=jnp.float32
                ).reshape(fold_size, width)
                * scale
            )
            value_part = jnp.einsum(
                "hqk,qhd->khd",
                probs.astype(jnp.bfloat16),
                grad_heads,
                preferred_element_type=jnp.float32,
            ).reshape(fold_size, width)
            key_grads = lax.dynamic_update_slice_in_dim(
                key_grads,
                lax.dynamic_slice_in_dim(key_grads, offset, fold_size, 0) + key_part,
                offset,
                0,
            )
            value_grads = lax.dynamic_update_slice_in_dim(
                value_grads,
                lax.dynamic_slice_in_dim(value_grads, offset, fold_size, 0) + value_part,
                offset,
                0,
            )
            return (query_grad, key_grads, value_grads)

        query_grad, key_grads, value_grads = lax.fori_loop(0, fold_count, fold_one, initial_back)
        key_grad, value_grad = (
            lax.psum_scatter(
                key_grads.astype(jnp.bfloat16), "seq", scatter_dimension=0, tiled=True
            ).astype(jnp.float32),
            lax.psum_scatter(
                value_grads.astype(jnp.bfloat16), "seq", scatter_dimension=0, tiled=True
            ).astype(jnp.float32),
        )
        query_share = query_grad.reshape(rows, width)
        d_queries = query_share.astype(jnp.bfloat16)
        d_keys = key_grad.astype(jnp.bfloat16)
        d_values = value_grad.astype(jnp.bfloat16)
        d_joined = jnp.concatenate([d_queries, d_keys, d_values], axis=1)
        grad_qvb = jnp.concatenate([column_sum(d_queries), column_sum(d_values)], axis=0)
        grad_qkv = left_trans(source, d_joined)
        input_grads.append(d_resid1 + right_trans(d_joined, back_qkv))
        terms = (
            grad_qkv,
            grad_qvb,
            grad_out_w,
            grad_outb,
            grad_g1,
            grad_b1,
            grad_up,
            grad_upb,
            grad_down,
            grad_downb,
            grad_g2,
            grad_b2,
        )
        if totals is None:
            totals = terms
        else:
            totals = tuple((first + second for first, second in zip(totals, terms)))
    shares = lax.psum_scatter(totals, ("dp", "seq"), scatter_dimension=0, tiled=True)
    layer_out = jnp.stack(outputs)[:, None]
    tokens_grad = jnp.stack(input_grads)[:, None]
    return (
        layer_out,
        tokens_grad,
        shares[0],
        shares[1],
        shares[2],
        shares[3],
        shares[4],
        shares[5],
        shares[6],
        shares[7],
        shares[8],
        shares[9],
        shares[10],
        shares[11],
    )


def solution(mesh):
    return jax.shard_map(
        on_device,
        mesh=mesh,
        in_specs=(
            P(None, "dp", "seq", None),
            P(None, "dp", None),
            P(("dp", "seq"), None),
            P(("dp", "seq")),
            P(("dp", "seq"), None),
            P(("dp", "seq")),
            P(("dp", "seq")),
            P(("dp", "seq")),
            P(("dp", "seq"), None),
            P(("dp", "seq")),
            P(("dp", "seq"), None),
            P(("dp", "seq")),
            P(("dp", "seq")),
            P(("dp", "seq")),
            P(None, "dp", "seq", None),
        ),
        out_specs=(
            P(None, "dp", "seq", None),
            P(None, "dp", "seq", None),
            P(("dp", "seq"), None),
            P(("dp", "seq")),
            P(("dp", "seq"), None),
            P(("dp", "seq")),
            P(("dp", "seq")),
            P(("dp", "seq")),
            P(("dp", "seq"), None),
            P(("dp", "seq")),
            P(("dp", "seq"), None),
            P(("dp", "seq")),
            P(("dp", "seq")),
            P(("dp", "seq")),
        ),
        check_vma=False,
    )
```

profile of v0, /device:TPU:0, one launch (start us, length us, event | category | flops | bytes accessed | tf_op | source)
XLA Modules:
  0.0 927.5 jit_solution(920579388821818816)
XLA Ops:
  16.8 42.6 %all-reduce.17 = (bf16[3072]{0:T(1024)(128)(2,1)S(1)}, bf16[1536]{0:T(1024)(128)(2,1)S(1)}, bf16[768]{0:T(1024)(128)(2,1)S(1)}, bf16[768]{0:T(1024)(128)(2,1)S(1...) all-reduce(bf16[3072]{0:T(1024)(128)(2,1)S(1)} %dynamic-update-slic, ...), channel_id=1, replica_groups=mesh['dp'=8,'seq'=4] {'dp','seq'}, use_global_device_ids=true, to_apply=%add.4 | all-reduce | flops 9216 | bytes 36864
  64.7 8.9 all-gather.5.cloned.1.call-done
  73.6 2.9 fusion.95
  77.7 12.7 %all_gather.34 = bf16[512,768]{1,0:T(8,128)(2,1)S(1)} all-gather(bf16[128,768]{1,0:T(8,128)(2,1)S(1)} %slice.119), channel_id=1, replica_groups=mesh['dp'=8,'seq'=4] {'seq'}, dimensions={0}, use_global_device_ids=true | all-gather | bytes 983040 | tf_op jit(solution)/shard_map/all_gather | solution.py:184
  91.6 10.5 %all_gather.35 = bf16[512,768]{1,0:T(8,128)(2,1)S(1)} all-gather(bf16[128,768]{1,0:T(8,128)(2,1)S(1)} %get-tuple-element.277), channel_id=1, replica_groups=mesh['dp'=8,'seq'=4] {'seq'}, dimensions={0}, use_global_device_ids=true | all-gather | bytes 983040 | tf_op jit(solution)/shard_map/all_gather | solution.py:185
  104.0 12.6 %all_gather.86 = bf16[512,768]{1,0:T(8,128)(2,1)S(1)} all-gather(bf16[128,768]{1,0:T(8,128)(2,1)S(1)} %slice.118), channel_id=1, replica_groups=mesh['dp'=8,'seq'=4] {'seq'}, dimensions={0}, use_global_device_ids=true | all-gather | bytes 983040 | tf_op jit(solution)/shard_map/all_gather | solution.py:184
  117.8 10.5 %all_gather.87 = bf16[512,768]{1,0:T(8,128)(2,1)S(1)} all-gather(bf16[128,768]{1,0:T(8,128)(2,1)S(1)} %get-tuple-element.271), channel_id=1, replica_groups=mesh['dp'=8,'seq'=4] {'seq'}, dimensions={0}, use_global_device_ids=true | all-gather | bytes 983040 | tf_op jit(solution)/shard_map/all_gather | solution.py:185
  143.0 52.9 %all-gather.9.cloned.1.call-done = bf16[768,3072]{1,0:T(8,128)(2,1)} async-done(((bf16[24,3072]{1,0:T(8,128)(2,1)}), bf16[768,3072]{1,0:T(8,128)(2,1)}) %all-gather.9.cloned.1.call-update) | async-done | bytes 4718608 | tf_op jit(solution)/shard_map/all_gather | solution.py:71
  195.9 9.0 multiply_convert_fusion.5
  204.9 55.6 %all-gather.11.cloned.1.call-done = bf16[3072,768]{1,0:T(8,128)(2,1)} async-done(((bf16[96,768]{1,0:T(8,128)(2,1)}), bf16[3072,768]{1,0:T(8,128)(2,1)}) %all-gather.11.cloned.1.call-update) | async-done | bytes 4718608 | tf_op jit(solution)/shard_map/all_gather | solution.py:73
  260.5 3.6 fusion.139
  264.6 5.5 multiply_convert_fusion.4
  278.9 2.5 convert_reduce_fusion
  281.4 3.1 convert_reduce_fusion.7
  289.1 3.6 fusion.33
  296.3 3.1 multiply_convert_fusion
  304.2 2.7 convolution_convert_fusion.1
  308.6 2.6 fusion.30
  323.9 2.5 convert_reduce_fusion.9
  329.0 19.7 %reduce-scatter.29.cloned.1.call-done = bf16[128,768]{1,0:T(8,128)(2,1)} async-done(((bf16[512,768]{1,0:T(8,128)(2,1)}), bf16[128,768]{1,0:T(8,128)(2,1)}) %reduce-scatter.29.cloned.1.call-update) | async-done | bytes 196624
  349.8 28.0 %reduce-scatter.27.cloned.1.call-done = bf16[128,768]{1,0:T(8,128)(2,1)} async-done(((bf16[512,768]{1,0:T(8,128)(2,1)}), bf16[128,768]{1,0:T(8,128)(2,1)}) %reduce-scatter.27.cloned.1.call-update) | async-done | bytes 196624
  378.9 28.0 %reduce-scatter.25.cloned.1.call-done = bf16[128,768]{1,0:T(8,128)(2,1)} async-done(((bf16[512,768]{1,0:T(8,128)(2,1)}), bf16[128,768]{1,0:T(8,128)(2,1)}) %reduce-scatter.25.cloned.1.call-update) | async-done | bytes 196624
  409.1 4.0 add_bitcast_fusion
  413.1 8.0 copy.87
  423.8 5.1 convolution_add_fusion.1
  431.6 5.1 convolution_add_fusion
  451.7 41.7 %all-reduce.16 = (f32[1536]{0:T(1024)}, f32[768]{0:T(1024)}, f32[768]{0:T(1024)}, f32[768]{0:T(1024)}, f32[3072]{0:T(1024)}, /*index=5*/f32[768]{0:T(1024)}, f32[768]{0:T(1024)}, f32[768]{0:T(1024)}) all-reduce(f32[1536]{0:T(1024)} %maximum_add_fusion, f32[768]{0:T(1024)S(1)} %add.424, ...), channel_id=7, replica_groups=mesh['dp'=8,'seq'=4] {'dp','seq'}, use_global_device_ids=true, to_apply=%region_35.36.clone | all-reduce | flops 9216 | bytes 73728
  503.6 2.6 fusion.56
  508.5 4.1 reduce-scatter.19.cloned.1.call-done
  512.6 124.7 %reduce-scatter.33.cloned.1.call-done = f32[24,2304]{1,0:T(8,128)} async-done(((f32[768,2304]{1,0:T(8,128)}), f32[24,2304]{1,0:T(8,128)}) %reduce-scatter.33.cloned.1.call-update) | async-done | bytes 221200
  637.3 141.6 %reduce-scatter.21.cloned.1.call-done = f32[24,3072]{1,0:T(8,128)} async-done(((f32[768,3072]{1,0:T(8,128)}), f32[24,3072]{1,0:T(8,128)}) %reduce-scatter.21.cloned.1.call-update) | async-done | bytes 294928 | tf_op jit(solution)/shard_map/reduce_scatter | solution.py:346
  778.9 141.5 %reduce-scatter.23.cloned.1.call-done = f32[96,768]{1,0:T(8,128)} async-done(((f32[3072,768]{1,0:T(8,128)}), f32[96,768]{1,0:T(8,128)}) %reduce-scatter.23.cloned.1.call-update) | async-done | bytes 294928 | tf_op jit(solution)/shard_map/reduce_scatter | solution.py:346
  (298 shorter events, 110.7 us)
Async XLA Ops:
  7.2 66.4 %all-gather.5.cloned.1.call-start = ((), (), s32[]{:S(2)}) async-start(), calls=%async_computation.8 | async-start | bytes 3649536 | tf_op jit(solution)/shard_map/all_gather | solution.py:65
  7.9 126.2 %all-gather.7.cloned.1.call-start = ((), (), s32[]{:S(2)}) async-start(), calls=%async_computation.9 | async-start | bytes 1216512 | tf_op jit(solution)/shard_map/all_gather | solution.py:67
  8.7 187.3 %all-gather.9.cloned.1.call-start = ((), (), s32[]{:S(2)}) async-start(), calls=%async_computation.10 | async-start | bytes 4866048 | tf_op jit(solution)/shard_map/all_gather | solution.py:71
  9.4 251.1 %all-gather.11.cloned.1.call-start = ((), (), s32[]{:S(2)}) async-start(), calls=%async_computation.11 | async-start | bytes 4866048 | tf_op jit(solution)/shard_map/all_gather | solution.py:73
  10.0 317.8 %reduce-scatter.31.cloned.1.call-start = ((), (), s32[]{:S(2)}) async-start(), calls=%async_computation.18 | async-start | bytes 983040
  64.7 11.9 %copy-start.22 = (bf16[2,1,128,768]{3,2,1,0:T(8,128)(2,1)S(1)}, bf16[2,1,128,768]{3,2,1,0:T(8,128)(2,1)}, u32[]{:S(2)}) copy-start(bf16[2,1,128,768]{3,2,1,0:T(8,128)(2,1)} %param.15) | copy-start | bytes 1179652
  73.6 3.2 copy-start.1
  77.7 51.8 %copy-start.42 = (bf16[128,768]{0,1:T(8,128)(2,1)}, bf16[128,768]{0,1:T(8,128)(2,1)S(1)}, u32[]{:S(2)}) copy-start(bf16[128,768]{0,1:T(8,128)(2,1)S(1)} %copy.68) | copy-start | bytes 589828
  260.5 4.0 copy-start.3
  260.5 9.6 %slice-start = ((s8[4718592]{0:T(1024)(128)(4,1)}), s8[4194304]{0:T(1024)(128)(4,1)S(1)}, s32[]{:S(2)}) async-start(s8[4718592]{0:T(1024)(128)(4,1)} %bitcast.187), calls=%async_computation.20 | async-start | bytes 8388608
  264.5 5.6 slice-start.1
  264.5 5.6 copy-start.11
  264.5 5.6 copy-start.54
  264.5 5.6 copy-start.62
  264.5 5.6 copy-start.66
  274.0 7.3 copy-start.25
  295.1 53.6 %reduce-scatter.29.cloned.1.call-start = ((), (), s32[]{:S(2)}) async-start(), calls=%async_computation.17 | async-start | bytes 983040
  296.3 4.3 copy-start.45
  304.1 73.7 %reduce-scatter.27.cloned.1.call-start = ((), (), s32[]{:S(2)}) async-start(), calls=%async_computation.16 | async-start | bytes 983040
  313.5 93.4 %reduce-scatter.25.cloned.1.call-start = ((), (), s32[]{:S(2)}) async-start(), calls=%async_computation.15 | async-start | bytes 983040
  314.6 3.3 copy-start.43
  319.6 193.0 %reduce-scatter.19.cloned.1.call-start = ((), (), s32[]{:S(2)}) async-start(), calls=%async_computation.12 | async-start | bytes 2433024 | tf_op jit(solution)/shard_map/reduce_scatter | solution.py:346
  322.5 3.9 copy-start.9
  322.5 314.8 %reduce-scatter.33.cloned.1.call-start = ((), (), s32[]{:S(2)}) async-start(), calls=%async_computation.19 | async-start | bytes 7299072
  326.4 81.5 %copy-start.24 = (bf16[2,1,128,768]{3,2,1,0:T(8,128)(2,1)S(1)}, bf16[2,1,128,768]{3,2,1,0:T(8,128)(2,1)}, u32[]{:S(2)}) copy-start(bf16[2,1,128,768]{3,2,1,0:T(8,128)(2,1)} %param.15) | copy-start | bytes 1179652
  327.8 81.3 %copy-start.48 = (bf16[12,64,128]{2,1,0:T(8,128)(2,1)}, bf16[12,64,128]{2,1,0:T(8,128)(2,1)S(1)}, u32[]{:S(2)}) copy-start(bf16[12,64,128]{2,1,0:T(8,128)(2,1)S(1)} %get-tuple-element.316) | copy-start | bytes 589828
  328.9 80.1 %copy-start.30 = (bf16[128,768]{0,1:T(8,128)(2,1)}, bf16[128,768]{0,1:T(8,128)(2,1)S(1)}, u32[]{:S(2)}) copy-start(bf16[128,768]{0,1:T(8,128)(2,1)S(1)} %copy.86) | copy-start | bytes 589828
  349.8 59.3 %copy-start.40 = (bf16[128,768]{0,1:T(8,128)(2,1)}, bf16[128,768]{0,1:T(8,128)(2,1)S(1)}, u32[]{:S(2)}) copy-start(bf16[128,768]{0,1:T(8,128)(2,1)S(1)} %copy.84) | copy-start | bytes 589828
  378.8 30.2 %copy-start.35 = (bf16[128,768]{0,1:T(8,128)(2,1)}, bf16[128,768]{0,1:T(8,128)(2,1)S(1)}, u32[]{:S(2)}) copy-start(bf16[128,768]{0,1:T(8,128)(2,1)S(1)} %copy.82) | copy-start | bytes 589828
  421.2 357.8 %reduce-scatter.21.cloned.1.call-start = ((), (), s32[]{:S(2)}) async-start(), calls=%async_computation.13 | async-start | bytes 9732096 | tf_op jit(solution)/shard_map/reduce_scatter | solution.py:346
  429.0 491.4 %reduce-scatter.23.cloned.1.call-start = ((), (), s32[]{:S(2)}) async-start(), calls=%async_computation.14 | async-start | bytes 9732096 | tf_op jit(solution)/shard_map/reduce_scatter | solution.py:346
  436.7 66.8 %copy-start.2 = (bf16[768,2304]{1,0:T(8,128)(2,1)S(1)}, bf16[768,2304]{1,0:T(8,128)(2,1)}, u32[]{:S(2)}) copy-start(bf16[768,2304]{1,0:T(8,128)(2,1)} %all-gather.5.cloned.1.call-done) | copy-start | bytes 10616836
  (52 other events, 93.2 us)
Sparse Core Ops, SparseCore 0:
  10.9 62.6 all-gather.4
  76.5 53.7 all-gather.6
  133.1 62.7 all-gather.8
  198.7 61.7 all-gather.10
  295.2 24.4 reduce-scatter.30
  322.5 26.1 reduce-scatter.28
  351.6 26.1 reduce-scatter.26
  380.7 26.1 reduce-scatter.24
  412.7 99.7 reduce-scatter.18
  518.7 118.5 reduce-scatter.32
  643.7 135.1 reduce-scatter.20
  785.2 135.0 reduce-scatter.22
where the time goes:
time: 934 us; the launch traced here: 927 us
  waiting for transfers between devices  608 us (65%)
  blocking collectives  131 us (14%)
  matrix products  86.2 us (9%)
  local copies, waits for them, and re-layouts  57.5 us (6%)
  other arithmetic  29.5 us (3%)
  between operations  15.3 us (2%)
    reduce_scatter x3, waiting for transfers between devices, on_device(): lax.psum_scatter(totals, ('dp', 'seq'), scatter_dimension=0, tiled=True)  287 us
    unnamed x17, waiting for transfers between devices  203 us
    unnamed x2, blocking collectives  84.3 us
    all_gather x1, waiting for transfers between devices, gather_forward(): lax.all_gather(shards[8], ('dp', 'seq'), axis=0, tiled=True)  55.6 us
    all_gather x1, waiting for transfers between devices, gather_forward(): lax.all_gather(shards[6], ('dp', 'seq'), axis=0, tiled=True)  52.9 us
    unnamed x177, local copies, waits for them, and re-layouts  46.3 us
    all_gather x2, blocking collectives, on_device(): key_piece = lax.all_gather(keys, 'seq', axis=0, tiled=True)  25.3 us
    dot_general x8, matrix products, matmul(): return jnp.dot(left, right, preferred_element_type=jnp.float32)  24.8 us
  transfers between devices with their start and end apart: 12, of which 10 were waited for; matrix products, arithmetic and copies ran while one was open for 14% of the time, Pallas kernels for 0%

commit v1 on v0

--- a/solution.py
+++ b/solution.py
@@ -1,8 +1,11 @@
+import functools
 import math
 
 import jax
 import jax.numpy as jnp
 from jax import lax
+from jax.experimental import pallas as pl
+from jax.experimental.pallas import tpu as pltpu
 from jax.sharding import PartitionSpec as P
 
 HEADS = 12
@@ -364,9 +367,373 @@
     )
 
 
+MESH = pl.DeviceIdType.MESH
+ZS, CS, YS, XS = 4, 2, 2, 2
+def place():
+    dp = lax.axis_index("dp"); seq = lax.axis_index("seq")
+    return dp // CS, dp % CS, seq // XS, seq % XS
+def dev(z, c, y, x):
+    return (z * CS + c, y * XS + x)
+def greet(z, c, y, x):
+    barrier = pltpu.get_barrier_semaphore()
+    partners = [dev((z + k) % ZS, c, y, x) for k in (1, 2, 3)]
+    partners += [dev(z, 1 - c, y, x), dev(z, c, 1 - y, x), dev(z, c, y, 1 - x)]
+    for p in partners:
+        pl.semaphore_signal(barrier, inc=1, device_id=p, device_id_type=MESH)
+    pl.semaphore_wait(barrier, len(partners))
+def gather_body(n, *refs):
+    ins, tok = refs[:n], refs[n]
+    outs, tout = refs[n + 1:2 * n + 1], refs[2 * n + 1]
+    (loc, zs, zr, xs, xr, ys, yr, as_, ar, bs, br, cs, cr, ts, tr) = refs[2 * n + 2:]
+    z, c, y, x = place()
+    X, Y = 1 - x, 1 - y
+    xn, yn, cn = dev(z, c, y, X), dev(z, c, Y, x), dev(z, 1 - c, y, x)
+    greet(z, c, y, x)
+    def rc(src, dst, s, r, d):
+        return pltpu.make_async_remote_copy(src_ref=src, dst_ref=dst, send_sem=s, recv_sem=r, device_id=d, device_id_type=MESH)
+    sent = []
+    def go(cp):
+        cp.start(); sent.append(cp)
+    local = []
+    for w in range(n):
+        cp = pltpu.make_async_copy(ins[w], outs[w].at[z, c, y, x], loc.at[w]); cp.start(); local.append(cp)
+    cp = pltpu.make_async_copy(tok, tout.at[y, x], loc.at[n]); cp.start(); local.append(cp)
+    for w in range(n):
+        o = outs[w].at[z, c, y, x]
+        for k in (1, 2, 3):
+            go(rc(ins[w], o, zs.at[w, k - 1], zr.at[w, k - 1], dev((z + k) % ZS, c, y, x)))
+        go(rc(ins[w], o, xs.at[w, 0], xr.at[w, 0], xn))
+        go(rc(ins[w], o, ys.at[w, 0], yr.at[w, 0], yn))
+        go(rc(ins[w], o, cs.at[w, 0, 0], cr.at[w, 0, 0], cn))
+    to = tout.at[y, x]
+    go(rc(tok, to, ts.at[0], tr.at[0], xn))
+    go(rc(tok, to, ts.at[1], tr.at[1], yn))
+    def half(w):
+        return ins[w].shape[-1] // 2
+    def relay(w, k):
+        q = (z + ZS - k) % ZS
+        bx, by = outs[w].at[q, c, y, X], outs[w].at[q, c, Y, x]
+        rc(bx, bx, xs.at[w, k], xr.at[w, k], xn).wait_recv()
+        h = half(w)
+        a = outs[w].at[q, c, y, X, :, pl.ds(0, h)]
+        go(rc(a, a, as_.at[w, k], ar.at[w, k], yn))
+        go(rc(bx, bx, cs.at[w, k, 1], cr.at[w, k, 1], cn))
+        rc(by, by, ys.at[w, k], yr.at[w, k], yn).wait_recv()
+        b = outs[w].at[q, c, Y, x, :, pl.ds(h, h)]
+        go(rc(b, b, bs.at[w, k], br.at[w, k], xn))
+        go(rc(by, by, cs.at[w, k, 2], cr.at[w, k, 2], cn))
+    for k in range(ZS):
+        if k:
+            for w in range(n):
+                q = (z + ZS - k) % ZS
+                o = outs[w].at[q, c, y, x]
+                rc(o, o, zs.at[w, k - 1], zr.at[w, k - 1], xn).wait_recv()
+                go(rc(o, o, xs.at[w, k], xr.at[w, k], xn))
+                go(rc(o, o, ys.at[w, k], yr.at[w, k], yn))
+                go(rc(o, o, cs.at[w, k, 0], cr.at[w, k, 0], cn))
+        for w in range(n):
+            relay(w, k)
+        if k == 0:
+            hh = tok.shape[-1] // 2
+            bx, by = tout.at[y, X], tout.at[Y, x]
+            rc(bx, bx, ts.at[0], tr.at[0], xn).wait_recv()
+            a = tout.at[y, X, :, :, pl.ds(0, hh)]
+            go(rc(a, a, ts.at[2], tr.at[2], yn))
+            rc(by, by, ts.at[1], tr.at[1], yn).wait_recv()
+            b = tout.at[Y, x, :, :, pl.ds(hh, hh)]
+            go(rc(b, b, ts.at[3], tr.at[3], xn))
+    for k in range(ZS):
+        q = (z + ZS - k) % ZS
+        for w in range(n):
+            h = half(w)
+            d = outs[w].at[q, c, Y, X]
+            a = outs[w].at[q, c, Y, X, :, pl.ds(0, h)]
+            b = outs[w].at[q, c, Y, X, :, pl.ds(h, h)]
+            rc(a, a, as_.at[w, k], ar.at[w, k], yn).wait_recv()
+            rc(b, b, bs.at[w, k], br.at[w, k], xn).wait_recv()
+            go(rc(d, d, cs.at[w, k, 3], cr.at[w, k, 3], cn))
+    hh = tok.shape[-1] // 2
+    a = tout.at[Y, X, :, :, pl.ds(0, hh)]
+    b = tout.at[Y, X, :, :, pl.ds(hh, hh)]
+    rc(a, a, ts.at[2], tr.at[2], yn).wait_recv()
+    rc(b, b, ts.at[3], tr.at[3], xn).wait_recv()
+    for k in range(ZS):
+        q = (z + ZS - k) % ZS
+        for w in range(n):
+            for j, (yy, xx) in enumerate(((y, x), (y, X), (Y, x), (Y, X))):
+                o = outs[w].at[q, 1 - c, yy, xx]
+                rc(o, o, cs.at[w, k, j], cr.at[w, k, j], cn).wait_recv()
+    for cp in sent:
+        cp.wait_send()
+    for cp in local:
+        cp.wait()
+def gather(shards, tok):
+    n = len(shards)
+    D = pltpu.SemaphoreType.DMA
+    outs = [jax.ShapeDtypeStruct((ZS, CS, YS, XS) + s.shape, s.dtype) for s in shards]
+    outs.append(jax.ShapeDtypeStruct((YS, XS) + tok.shape, tok.dtype))
+    res = pl.pallas_call(
+        functools.partial(gather_body, n),
+        out_shape=outs,
+        in_specs=[pl.BlockSpec(memory_space=pltpu.VMEM)] * (n + 1),
+        out_specs=[pl.BlockSpec(memory_space=pl.ANY)] * (n + 1),
+        scratch_shapes=[D((n + 1,)), D((n, 3)), D((n, 3)), D((n, 4)), D((n, 4)), D((n, 4)), D((n, 4)), D((n, 4)), D((n, 4)), D((n, 4)), D((n, 4)), D((n, 4, 4)), D((n, 4, 4)), D((4,)), D((4,))],
+        compiler_params=pltpu.CompilerParams(collective_id=0, has_side_effects=True),
+        name="gather",
+    )(*shards, tok)
+    return res[:n], res[n]
+
+def scatter_body(n, *refs):
+    gs, tp, base = refs[:n], refs[n], refs[n + 1]
+    outs, tout = refs[n + 2:2 * n + 2], refs[2 * n + 2]
+    k = 2 * n + 3
+    hs, rbs, ras, rys, r2as, r2bs, rzs = (refs[k + i * n:k + (i + 1) * n] for i in range(7))
+    k += 7 * n
+    (tx, ty, t2a, t2b, own, loc, ss, sr, tss, tsr, tl) = refs[k:]
+    z, c, y, x = place()
+    X, Y = 1 - x, 1 - y
+    xn, yn, cn = dev(z, c, y, X), dev(z, c, Y, x), dev(z, 1 - c, y, x)
+    greet(z, c, y, x)
+    def rc(src, dst, s, r, d):
+        return pltpu.make_async_remote_copy(src_ref=src, dst_ref=dst, send_sem=s, recv_sem=r, device_id=d, device_id_type=MESH)
+    sent = []
+    def go(cp):
+        cp.start(); sent.append(cp)
+    half = [h.shape[-1] // 2 for h in hs]
+    A = [pl.ds(0, h) for h in half]
+    B = [pl.ds(h, h) for h in half]
+    f32 = jnp.float32
+    def swap(w):
+        return rc(gs[w].at[:, 1 - c], rbs[w], ss.at[w, 0], sr.at[w, 0], cn)
+    def load(w):
+        return pltpu.make_async_copy(gs[w].at[:, c], hs[w], loc.at[w])
+    for w in range(n):
+        load(w).start()
+        go(swap(w))
+    hh = tp.shape[-1] // 2
+    TA, TB = pl.ds(0, hh), pl.ds(hh, hh)
+    tload = pltpu.make_async_copy(tp, own, tl.at[0])
+    tload.start()
+    go(rc(tp.at[:, X, :, :, TA], tx, tss.at[0], tsr.at[0], xn))
+    go(rc(tp.at[Y, :, :, :, TB], ty, tss.at[1], tsr.at[1], yn))
+    def s1a(w): return rc(hs[w].at[:, :, X, :, A[w]], ras[w], ss.at[w, 1], sr.at[w, 1], xn)
+    def s1b(w): return rc(hs[w].at[:, Y, :, :, B[w]], rys[w], ss.at[w, 2], sr.at[w, 2], yn)
+    def s2a(w): return rc(hs[w].at[:, Y, x, :, A[w]], r2as[w], ss.at[w, 3], sr.at[w, 3], yn)
+    def s2b(w): return rc(hs[w].at[:, y, X, :, B[w]], r2bs[w], ss.at[w, 4], sr.at[w, 4], xn)
+    def s3(w, k): return rc(hs[w].at[(z + k) % ZS, y, x], rzs[w].at[k - 1], ss.at[w, 4 + k], sr.at[w, 4 + k], dev((z + k) % ZS, c, y, x))
+    def st0(w):
+        load(w).wait()
+        swap(w).wait_recv()
+        def one(i, _):
+            for yy in range(YS):
+                for xx in range(XS):
+                    hs[w][i, yy, xx] = (hs[w][i, yy, xx].astype(f32) + rbs[w][i, yy, xx].astype(f32)).astype(jnp.bfloat16)
+            return 0
+        lax.fori_loop(0, ZS, one, 0)
+        go(s1a(w)); go(s1b(w))
+    def st1(w):
+        s1a(w).wait_recv(); s1b(w).wait_recv()
+        def one(i, _):
+            for j in range(2):
+                hs[w][i, j, x, :, A[w]] = (hs[w][i, j, x, :, A[w]].astype(f32) + ras[w][i, j].astype(f32)).astype(jnp.bfloat16)
+                hs[w][i, y, j, :, B[w]] = (hs[w][i, y, j, :, B[w]].astype(f32) + rys[w][i, j].astype(f32)).astype(jnp.bfloat16)
+            return 0
+        lax.fori_loop(0, ZS, one, 0)
+        go(s2a(w)); go(s2b(w))
+    def st2(w):
+        s2a(w).wait_recv(); s2b(w).wait_recv()
+        def one(i, _):
+            hs[w][i, y, x, :, A[w]] = (hs[w][i, y, x, :, A[w]].astype(f32) + r2as[w][i].astype(f32)).astype(jnp.bfloat16)
+            hs[w][i, y, x, :, B[w]] = (hs[w][i, y, x, :, B[w]].astype(f32) + r2bs[w][i].astype(f32)).astype(jnp.bfloat16)
+            return 0
+        lax.fori_loop(0, ZS, one, 0)
+        for k in (1, 2, 3):
+            go(s3(w, k))
+    def st3(w):
+        total = hs[w][z, y, x].astype(f32)
+        for k in (1, 2, 3):
+            s3(w, k).wait_recv()
+            total = total + rzs[w][k - 1].astype(f32)
+        outs[w][...] = total
+    def t1():
+        tload.wait()
+        rc(tx, tx, tss.at[0], tsr.at[0], xn).wait_recv()
+        rc(ty, ty, tss.at[1], tsr.at[1], yn).wait_recv()
+        own[Y, x, :, :, TA] = (own[Y, x, :, :, TA].astype(f32) + tx[Y].astype(f32)).astype(jnp.bfloat16)
+        own[y, X, :, :, TB] = (own[y, X, :, :, TB].astype(f32) + ty[X].astype(f32)).astype(jnp.bfloat16)
+        go(rc(own.at[Y, x, :, :, TA], t2a, tss.at[2], tsr.at[2], yn))
+        go(rc(own.at[y, X, :, :, TB], t2b, tss.at[3], tsr.at[3], xn))
+    def t2():
+        rc(t2a, t2a, tss.at[2], tsr.at[2], yn).wait_recv()
+        rc(t2b, t2b, tss.at[3], tsr.at[3], xn).wait_recv()
+        tout[:, :, TA] = base[:, :, TA] + tx[y].astype(f32) + t2a[...].astype(f32)
+        tout[:, :, TB] = base[:, :, TB] + ty[x].astype(f32) + t2b[...].astype(f32)
+    for t in range(n + 4):
+        for s, f in enumerate((st0, st1, st2, st3)):
+            if 0 <= t - s < n:
+                f(t - s)
+        if t == 1: t1()
+        if t == n + 1: t2()
+    for cp in sent:
+        cp.wait_send()
+
+def scatter(grads, tpart, base):
+    n = len(grads)
+    D = pltpu.SemaphoreType.DMA
+    V = pltpu.VMEM
+    bf = jnp.bfloat16
+    outs = [jax.ShapeDtypeStruct(g.shape[4:], jnp.float32) for g in grads] + [jax.ShapeDtypeStruct(base.shape, jnp.float32)]
+    rn = [g.shape[4:] for g in grads]
+    scr = [V((ZS, YS, XS, r, m), bf) for r, m in rn]
+    scr += [V((ZS, YS, XS, r, m), bf) for r, m in rn]
+    scr += [V((ZS, 2, r, m // 2), bf) for r, m in rn] * 2
+    scr += [V((ZS, r, m // 2), bf) for r, m in rn] * 2
+    scr += [V((ZS - 1, r, m), bf) for r, m in rn]
+    ts = tpart.shape[2:]
+    th = (ts[0], ts[1], ts[2] // 2)
+    scr += [V((2,) + th, bf)] * 2 + [V(th, bf)] * 2 + [V(tpart.shape, bf)]
+    scr += [D((n,)), D((n, 8)), D((n, 8)), D((4,)), D((4,)), D((1,))]
+    res = pl.pallas_call(
+        functools.partial(scatter_body, n),
+        out_shape=outs,
+        in_specs=[pl.BlockSpec(memory_space=pl.ANY)] * (n + 1) + [pl.BlockSpec(memory_space=V)],
+        out_specs=[pl.BlockSpec(memory_space=V)] * (n + 1),
+        scratch_shapes=scr,
+        compiler_params=pltpu.CompilerParams(collective_id=1, has_side_effects=True, vmem_limit_bytes=60 * 2**20),
+        name="scatter",
+    )(*grads, tpart, base)
+    return res[:n], res[n]
+
+
+def fits(mesh):
+    return mesh.shape["dp"] == ZS * CS and mesh.shape["seq"] == YS * XS
+
+
+def pack(parts, shape):
+    joined = jnp.concatenate(parts, axis=-1)
+    size = shape[-1] * shape[-2]
+    pad = [(0, 0)] * (joined.ndim - 1) + [(0, size - joined.shape[-1])]
+    return jnp.pad(joined, pad).reshape(joined.shape[:-1] + shape)
+
+
+def fast_device(
+    tokens, piece_starts, qkv_weight, qv_bias, out_weight, out_bias, norm1_gain, norm1_bias,
+    up_weight, up_bias, down_weight, down_bias, norm2_gain, norm2_bias, grad_out,
+):
+    f32, bf16 = jnp.float32, jnp.bfloat16
+    micro_count, _, rows, width = tokens.shape
+    head_size = width // HEADS
+    scale = 1.0 / math.sqrt(head_size)
+    ranks = YS * XS
+    length = rows * ranks
+    count = micro_count * rows
+    small = (qv_bias, out_bias, norm1_gain, norm1_bias, up_bias, down_bias, norm2_gain, norm2_bias)
+    widths = [v.shape[0] for v in small]
+    vector = pack(small, (8, 256))
+    gathered, tok = gather((qkv_weight, out_weight, up_weight, down_weight, vector), tokens[:, 0])
+    wqkv, wout, wup, wdown = (g.reshape(-1, g.shape[-1]) for g in gathered[:4])
+    flat = gathered[4].reshape(-1, 8 * 256).astype(f32)
+    full, at = [], 0
+    for w in widths:
+        full.append(flat[:, at : at + w].reshape(-1))
+        at += w
+    qvb, outb, g1, b1, upb, downb, g2, b2 = full
+    tok_all = tok.reshape(ranks, micro_count, rows, width).transpose(1, 0, 2, 3)
+    tok_all = tok_all.reshape(micro_count * length, width)
+    me = lax.axis_index("seq")
+    query_pos = me * rows + jnp.arange(rows, dtype=jnp.int32)
+    key_pos = jnp.arange(length, dtype=jnp.int32)
+    allowed = jnp.stack(
+        [
+            visible_mask(query_pos, owners(query_pos, s), key_pos, owners(key_pos, s))
+            for s in (piece_starts[m, 0] for m in range(micro_count))
+        ]
+    )
+    source = tokens.reshape(count, width)
+    queries = (matmul(source, wqkv[:, :width]) + qvb[:width]).astype(bf16)
+    kv = matmul(tok_all, wqkv[:, width:])
+    keys = kv[:, :width].astype(bf16)
+    values = (kv[:, width:] + qvb[width:]).astype(bf16)
+    qh = queries.reshape(micro_count, rows, HEADS, head_size)
+    kh = keys.reshape(micro_count, length, HEADS, head_size)
+    vh = values.reshape(micro_count, length, HEADS, head_size)
+
+    def dot(eq, a, b):
+        return jnp.einsum(eq, a, b, preferred_element_type=f32)
+
+    scores = jnp.where(allowed[:, None], dot("mqhd,mkhd->mhqk", qh, kh) * scale, NEG)
+    expo = jnp.exp(scores - jnp.max(scores, axis=-1, keepdims=True))
+    probs = expo / jnp.sum(expo, axis=-1, keepdims=True)
+    probs_low = probs.astype(bf16)
+    attended = dot("mhqk,mkhd->mqhd", probs_low, vh).reshape(count, width).astype(bf16)
+    resid1 = source.astype(f32) + matmul(attended, wout) + outb
+    normed1, inverse1 = normalize(resid1)
+    mixed1 = normed1 * g1 + b1
+    inner = mixed1.astype(bf16)
+    pre = matmul(inner, wup) + upb
+    act, gelu_back = jax.vjp(lambda v: jax.nn.gelu(v, approximate=False), pre)
+    act = act.astype(bf16)
+    resid2 = mixed1 + matmul(act, wdown) + downb
+    normed2, inverse2 = normalize(resid2)
+    layer_out = (normed2 * g2 + b2).astype(bf16)
+    cotan = grad_out.reshape(count, width).astype(f32)
+    d_resid2 = norm_back(cotan, normed2, inverse2, g2)
+    d_branch2 = d_resid2.astype(bf16)
+    grad_down = left_trans(act, d_branch2)
+    d_pre = gelu_back(right_trans(d_branch2, wdown))[0].astype(bf16)
+    grad_up = left_trans(inner, d_pre)
+    d_mixed1 = d_resid2 + right_trans(d_pre, wup)
+    d_resid1 = norm_back(d_mixed1, normed1, inverse1, g1)
+    d_branch1 = d_resid1.astype(bf16)
+    grad_out_w = left_trans(attended, d_branch1)
+    d_attended = right_trans(d_branch1, wout).astype(bf16)
+    dh = d_attended.reshape(micro_count, rows, HEADS, head_size)
+    d_probs = dot("mqhd,mkhd->mhqk", dh, vh)
+    delta = jnp.sum(probs * d_probs, axis=-1, keepdims=True)
+    d_scores = (probs * (d_probs - delta)).astype(bf16)
+    d_queries = (dot("mhqk,mkhd->mqhd", d_scores, kh) * scale).reshape(count, width).astype(bf16)
+    d_keys = dot("mhqk,mqhd->mkhd", d_scores, qh) * scale
+    d_values = dot("mhqk,mqhd->mkhd", probs_low, dh)
+    d_kv = jnp.concatenate(
+        [d_keys.reshape(-1, width).astype(bf16), d_values.reshape(-1, width).astype(bf16)], axis=1
+    )
+    grad_qkv = jnp.concatenate([left_trans(source, d_queries), left_trans(tok_all, d_kv)], axis=1)
+    part = right_trans(d_kv, wqkv[:, width:]).reshape(micro_count, ranks, rows, width)
+    own = lax.dynamic_index_in_dim(part, me, 1, keepdims=False)
+    base = (d_resid1 + right_trans(d_queries, wqkv[:, :width])).reshape(micro_count, rows, width) + own
+    part = part.astype(bf16).transpose(1, 0, 2, 3).reshape(YS, XS, micro_count, rows, width)
+    terms = (
+        jnp.concatenate([column_sum(d_queries), column_sum(d_kv[:, width:])]),
+        column_sum(d_branch1),
+        jnp.sum(d_mixed1 * normed1, axis=0),
+        jnp.sum(d_mixed1, axis=0),
+        column_sum(d_pre),
+        column_sum(d_branch2),
+        jnp.sum(cotan * normed2, axis=0),
+        jnp.sum(cotan, axis=0),
+    )
+    vec_grad = pack([t.reshape(-1, w) for t, w in zip(terms, widths)], (8, 256))
+    grads = [
+        g.astype(bf16).reshape((ZS, CS, YS, XS, -1, g.shape[-1]))
+        for g in (grad_down, grad_up, grad_out_w, grad_qkv)
+    ]
+    grads.append(vec_grad.astype(bf16).reshape(ZS, CS, YS, XS, 8, 256))
+    shares, tokens_grad = scatter(grads, part, base)
+    flat = shares[4].reshape(-1)
+    vec, at = [], 0
+    for w in widths:
+        vec.append(flat[at : at + w])
+        at += w
+    return (
+        layer_out.reshape(tokens.shape), tokens_grad.reshape(tokens.shape),
+        shares[3], vec[0], shares[2], vec[1], vec[2], vec[3], shares[1], vec[4], shares[0],
+        vec[5], vec[6], vec[7],
+    )
+
+
 def solution(mesh):
     return jax.shard_map(
-        on_device,
+        fast_device if fits(mesh) else on_device,
         mesh=mesh,
         in_specs=(
             P(None, "dp", "seq", None),

time: 934 us -> 349 us (0.37)
  waiting for transfers between devices: 608 us -> 0 us
  Pallas kernels: 0 us -> 176 us
  blocking collectives: 131 us -> 0 us
  between operations: 15.3 us -> 1.44 us
    reduce_scatter x3 -> x0, waiting for transfers between devices: 287 us -> none  [on_device(): lax.psum_scatter(totals, ('dp', 'seq'), scatter_dimension=0, tiled=True)]
    unnamed x17 -> x0, waiting for transfers between devices: 203 us -> none
    pallas_call x0 -> x2, Pallas kernels: none -> 176 us  [the longest x1 92.4 us: scatter(): pl.pallas_call(functools.partial(scatter_body, n), out_shape=outs, in_spe...]
    all_gather x4 -> x0, waiting for transfers between devices: 117 us -> none  [the longest x1 55.6 us: gather_forward(): lax.all_gather(shards[8], ('dp', 'seq'), axis=0, tiled=True)]
    unnamed x2 -> x0, blocking collectives: 84.3 us -> none
    all_gather x4 -> x0, blocking collectives: 46.3 us -> none  [the longest x2 25.3 us: on_device(): key_piece = lax.all_gather(keys, 'seq', axis=0, tiled=True)]
    unnamed x177 -> x74, local copies, waits for them, and re-layouts: 46.3 us -> 15.3 us
    reshape x0 -> x14, local copies, waits for them, and re-layouts: none -> 17.9 us  [the longest x7 8.33 us: fast_device(): vec_grad = pack([t.reshape(-1, w) for t, w in zip(terms, widths)], (8, 256))]
  transfers between devices with their start and end apart: 12 -> 0, of which waited for: 10 -> 0; matrix products, arithmetic and copies ran while one was open for 14% -> 0% of each run, Pallas kernels for 0% -> 0%
where the time goes in v1:
time: 349 us; the launch traced here: 343 us
  Pallas kernels  176 us (50%)
  matrix products  77.9 us (22%)
  local copies, waits for them, and re-layouts  62.9 us (18%)
  other arithmetic  24.9 us (7%)
    pallas_call x1, Pallas kernels, scatter(): pl.pallas_call(functools.partial(scatter_body, n), out_shape=outs, in_spe...  92.4 us
    pallas_call x1, Pallas kernels, gather(): pl.pallas_call(functools.partial(gather_body, n), out_shape=outs, in_spec...  83.4 us
    dot_general x5, matrix products, matmul(): return jnp.dot(left, right, preferred_element_type=jnp.float32)  24.7 us
    dot_general x5, matrix products, right_trans(): lax.dot_general(left, right, (((1,), (1,)), ((), ())), preferred_element_...  19.7 us
    dot_general x6, matrix products, dot(): return jnp.einsum(eq, a, b, preferred_element_type=f32)  16.9 us
    dot_general x5, matrix products, left_trans(): lax.dot_general(left, right, (((0,), (0,)), ((), ())), preferred_element_...  16.5 us
    unnamed x74, local copies, waits for them, and re-layouts  15.3 us
    reshape x7, local copies, waits for them, and re-layouts, fast_device(): vec_grad = pack([t.reshape(-1, w) for t, w in zip(terms, widths)], (8, 256))  8.33 us

profile of v1, /device:TPU:0, one launch (start us, length us, event | category | flops | bytes accessed | tf_op | source)
XLA Modules:
  0.0 342.9 jit_solution(12805723456330548631)
XLA Ops:
  3.1 5.4 %concatenate.26 = bf16[288]{0:T(512)(128)(2,1)S(1)} concatenate(bf16[48]{0:T(256)(128)(2,1)} %param.18, bf16[24]{0:T(256)(128)(2,1)} %param.20, bf16[24]{0:T(256)(128)(2,1)} %param.21, bf16[24]{0:T(256)(128)(2,1)} %param.22, bf16[96]{0:T(256)(128)(2,1)} %param.24, bf16[24]{0:T(256)(128)(2,1)} %param.26, bf16[24]{0:T(256)(128)(2,1)} %param.27, bf16[24]{0:T(256)(128)(2,1)} %param.28), dimensions={0} | concatenate | bytes 1152 | tf_op jit(solution)/shard_map/concatenate | solution.py:613
  9.1 83.4 %gather.1 = (bf16[4,2,2,2,24,2304]{5,4,3,2,1,0:T(8,128)(2,1)}, bf16[4,2,2,2,24,768]{5,4,3,2,1,0:T(8,128)(2,1)}, bf16[4,2,2,2,24,3072]{5,4,3,2,1,0:T(8,128)(2,1)}...) custom-call(bf16[24,2304]{1,0:T(8,128)(2,1)} %refs_0_.1, ...), custom_call_target="tpu_custom_call" | custom-call | tf_op jit(solution)/shard_map/gather/pallas_call | solution.py:475
  94.4 1.9 fusion.50
  96.5 4.8 %fusion.15 = f32[1024,1536]{1,0:T(8,128)S(1)} fusion(bf16[1024,768]{1,0:T(8,128)(2,1)S(1)} %bitcast.137, bf16[768,2304]{1,0:T(8,128)(2,1)} %bitcast.169), kind=kOutput, calls=%fused_computation.40 | convolution fusion | flops 2415919104 | bytes 10223616 | tf_op jit(solution)/shard_map/dot_general | solution.py:46
  101.4 2.6 copy-done.7
  107.8 4.4 %fusion.97 = (f32[2,12,128]{2,1,0:T(8,128)S(1)}, f32[2,12,128,512]{3,2,1,0:T(8,128)}) fusion(f32[2,12,128,512]{3,2,1,0:T(8,128)S(1)} %fusion.26, pred[2,128,512]{2,1,0:T(8,128)(4,1)S(1)} %copy-done.20), kind=kOutput, calls=%fused_computation.150 | output fusion | flops 9437695 | bytes 12726272 | tf_op jit(solution)/shard_map/sub | solution.py:665
  112.3 3.3 fusion.3
  117.3 2.4 reshape.445
  119.7 4.6 %fusion.42 = bf16[2,128,12,64]{1,3,2,0:T(8,128)(2,1)S(1)} fusion(bf16[2,512,12,64]{1,0,3,2:T(2,128)(2,1)} %reshape.445, f32[2,12,128,512]{3,2,1,0:T(8,128)} %get-tuple-element.130, f32[2,12,128]{2,1,0:T(8,128)S(1)} %get-tuple-element.129), kind=kOutput, calls=%fused_computation.68 | convolution fusion | flops 204668928 | bytes 8269824 | tf_op jit(solution)/shard_map/mhqk,mkhd->mqhd/dot_general | solution.py:662
  126.5 1.9 fusion.98
  129.7 11.8 %multiply_convert_fusion.2 = (bf16[256,3072]{1,0:T(8,128)(2,1)}, f32[256,3072]{1,0:T(8,128)}, f32[256,3072]{1,0:T(8,128)}) fusion(f32[3072]{0:T(1024)S(1)} %add.156, bf16[768,3072]{1,0:T(8,128)(2,1)} %bitcast.178, f32[256,768]{1,0:T(8,128)S(1)} %get-tuple-element.132, f32[768]{0:T(1024)S(1)} %add.153, f32[768]{0:T(1024)S(1)} %mul.164, ...), kind=kOutput, calls=%fused_computation.20 | convolution fusion | flops 1260847104 | bytes 13389824 | tf_op jit(solution)/shard_map/dot_general | solution.py:46
  142.2 4.4 %fusion.99 = (f32[256]{0:T(256)S(1)}, f32[256,768]{1,0:T(8,128)S(1)}) fusion(f32[768]{0:T(1024)} %add.160, bf16[256,3072]{1,0:T(8,128)(2,1)} %get-tuple-element.106, bf16[3072,768]{1,0:T(8,128)(2,1)} %bitcast.182, f32[768]{0:T(1024)S(1)} %add.153, f32[768]{0:T(1024)S(1)} %mul.164, f32[256]{0:T(256)S(1)} %add_rsqrt_fusion.1, ...), kind=kOutput, calls=%fused_computation.152 | convolution fusion | flops 1209335552 | bytes 7876608 | tf_op jit(solution)/shard_map/dot_general | solution.py:46
  149.6 2.5 fusion.59
  154.0 6.4 %fusion.102 = (bf16[3072]{0:T(1024)(128)(2,1)}, bf16[256,3072]{1,0:T(8,128)(2,1)S(1)}) fusion(f32[256,3072]{1,0:T(8,128)S(1)} %copy-done.29, f32[256,3072]{1,0:T(8,128)} %get-tuple-element.133, bf16[3072,768]{1,0:T(8,128)(2,1)} %bitcast.183, f32[256,768]{1,0:T(8,128)S(1)} %get-tuple-element.103), kind=kOutput, calls=%fused_computation.155 | convolution fusion | flops 1219949568 | bytes 13375488 | tf_op jit(solution)/shard_map/dot_general | solution.py:56
  160.5 2.2 multiply_reduce_fusion.1
  164.8 1.9 copy.94
  166.8 1.8 reshape.455
  168.6 5.1 %multiply_reduce_fusion = (f32[2,12,128]{2,1,0:T(8,128)S(1)}, f32[2,12,128,512]{3,2,1,0:T(8,128)S(1)}) fusion(f32[2,12,128,512]{3,2,1,0:T(8,128)} %get-tuple-element.130, f32[2,12,128]{2,1,0:T(8,128)} %copy-done.24, bf16[2,512,12,64]{1,0,3,2:T(2,128)(2,1)} %reshape.445, bf16[2,128,12,64]{1,0,3,2:T(2,128)(2,1)} %reshape.455), kind=kOutput, calls=%fused_computation.2 | convolution fusion | flops 206042112 | bytes 14573568 | tf_op jit(solution)/shard_map/mqhd,mkhd->mhqk/dot_general | solution.py:662
  173.7 3.6 %multiply_convert_fusion = bf16[2,12,128,512]{3,2,1,0:T(8,128)(2,1)S(1)} fusion(f32[2,12,128,512]{3,2,1,0:T(8,128)S(1)} %get-tuple-element.138, f32[2,12,128]{2,1,0:T(8,128)S(1)} %get-tuple-element.137, f32[2,12,128,512]{3,2,1,0:T(8,128)} %get-tuple-element.130, f32[2,12,128]{2,1,0:T(8,128)S(1)} %copy-done.25), kind=kLoop, calls=%fused_computation.1 | loop fusion | flops 6291456 | bytes 15753216 | tf_op jit(solution)/shard_map/convert_element_type | solution.py:693
  179.1 2.8 convolution_add_fusion.1
  186.2 4.3 %fusion.100 = (bf16[12,64]{1,0:T(8,128)(2,1)}, bf16[2,12,64,512]{3,2,1,0:T(8,128)(2,1)S(1)}) fusion(f32[2,12,128,512]{3,2,1,0:T(8,128)} %get-tuple-element.130, f32[2,12,128]{2,1,0:T(8,128)} %copy-done.24, bf16[2,128,12,64]{1,0,3,2:T(2,128)(2,1)} %reshape.455), kind=kOutput, calls=%fused_computation.153 | convolution fusion | flops 206044416 | bytes 8271360 | tf_op jit(solution)/shard_map/mhqk,mqhd->mkhd/dot_general | solution.py:662
  194.1 7.0 %fusion.13 = f32[1024,768]{1,0:T(8,128)} fusion(bf16[768,2304]{1,0:T(8,128)(2,1)} %bitcast.171, bf16[1024,768]{1,0:T(8,128)(2,1)} %copy.105, bf16[1024,768]{1,0:T(8,128)(2,1)} %copy.104), kind=kOutput, calls=%fused_computation.38 | convolution fusion | flops 2422210560 | bytes 8650752 | tf_op jit(solution)/shard_map/dot_general | solution.py:56
  201.1 2.1 bitcast_add_fusion.refs_6_
  203.2 3.4 copy.161
  218.7 2.6 convolution_convert_fusion.4
  221.3 1.9 copy.99
  223.2 5.1 %convolution_convert_fusion.2 = bf16[4,2,2,2,24,1536]{5,4,3,2,1,0:T(8,128)(2,1)S(1)} fusion(bf16[4,2,2,2,24,1024]{5,4,3,2,1,0:T(8,128)(2,1)} %bitcast.153, bf16[1024,768]{1,0:T(8,128)(2,1)} %copy.105, bf16[1024,768]{1,0:T(8,128)(2,1)} %copy.104), kind=kOutput, calls=%fused_computation.11 | convolution fusion | flops 2423390208 | bytes 7077888 | tf_op jit(solution)/shard_map/dot_general | solution.py:50
  228.3 2.0 pad_maximum_fusion.refs_3_
  231.9 3.7 %convolution_convert_fusion = bf16[768,3072]{1,0:T(8,128)(2,1)} fusion(bf16[256,3072]{1,0:T(8,128)(2,1)S(1)} %copy-done.17, f32[256,768]{1,0:T(8,128)S(1)} %get-tuple-element.132, f32[768]{0:T(1024)S(1)} %add.153, f32[768]{0:T(1024)S(1)} %mul.164, f32[256]{0:T(256)S(1)} %copy-done.28, f32[256]{0:T(256)S(1)} %copy-done.22), kind=kOutput, calls=%fused_computation.5 | convolution fusion | flops 1211301888 | bytes 7086080 | tf_op jit(solution)/shard_map/dot_general | solution.py:50
  235.6 3.6 %convolution_convert_fusion.1 = bf16[3072,768]{1,0:T(8,128)(2,1)} fusion(bf16[256,3072]{1,0:T(8,128)(2,1)S(1)} %copy-done.6, f32[256,768]{1,0:T(8,128)S(1)} %copy-done.10), kind=kOutput, calls=%fused_computation.6 | convolution fusion | flops 1210515456 | bytes 7077888 | tf_op jit(solution)/shard_map/dot_general | solution.py:50
  239.3 92.4 %scatter.1 = (f32[96,768]{1,0:T(8,128)}, f32[24,3072]{1,0:T(8,128)}, f32[24,768]{1,0:T(8,128)}, f32[24,2304]{1,0:T(8,128)}, f32[8,256]{1,0:T(8,128)}, /*index=5*/f32[2,128,768]{2,1,0:T(8,128)}) custom-call(bf16[4,2,2,2,96,768]{5,4,3,2,1,0:T(8,128)(2,1)} %bitcast.135, bf16[4,2,2,2,24,3072]{5,4,3,2,1,0:T(8,128)(2,1)} %bitcast.136, ...), custom_call_target="tpu_custom_call" | custom-call | tf_op jit(solution)/shard_map/scatter/pallas_call | solution.py:596
  334.0 2.1 copy.179
  (141 shorter events, 53.9 us)
Async XLA Ops:
  92.5 3.8 %copy-start.12 = (bf16[2,2,2,128,768]{4,3,2,1,0:T(8,128)(2,1)S(1)}, bf16[2,2,2,128,768]{4,3,2,1,0:T(8,128)(2,1)}, u32[]{:S(2)}) copy-start(bf16[2,2,2,128,768]{4,3,2,1,0:T(8,128)(2,1)} %get-tuple-element.26) | copy-start | bytes 4718596
  93.6 0.7 copy-start.19
  96.4 10.3 %copy-start.4 = (bf16[2,128,12,64]{1,0,3,2:T(2,128)(2,1)}, bf16[2,128,12,64]{1,0,3,2:T(2,128)(2,1)S(1)}, u32[]{:S(2)}) copy-start(bf16[2,128,12,64]{1,0,3,2:T(2,128)(2,1)S(1)} %reshape.446) | copy-start | bytes 1179652
  96.5 4.8 %copy-start = (bf16[4,2,128,768]{3,2,0,1:T(8,128)(2,1)}, bf16[4,2,128,768]{3,2,0,1:T(8,128)(2,1)S(1)}, u32[]{:S(2)}) copy-start(bf16[4,2,128,768]{3,2,0,1:T(8,128)(2,1)S(1)} %copy.87) | copy-start | bytes 4718596
  101.4 2.7 copy-start.7
  106.7 1.0 copy-start.20
  112.2 7.5 %copy-start.24 = (f32[2,12,128]{2,1,0:T(8,128)}, f32[2,12,128]{2,1,0:T(8,128)S(1)}, u32[]{:S(2)}) copy-start(f32[2,12,128]{2,1,0:T(8,128)S(1)} %get-tuple-element.129) | copy-start | bytes 36868
  119.7 6.8 %copy-start.15 = (bf16[2,1,128,768]{3,2,1,0:T(8,128)(2,1)S(1)}, bf16[2,1,128,768]{3,2,1,0:T(8,128)(2,1)}, u32[]{:S(2)}) copy-start(bf16[2,1,128,768]{3,2,1,0:T(8,128)(2,1)} %param.15) | copy-start | bytes 1179652
  124.7 16.7 %copy-start.13 = (bf16[2,128,12,64]{1,0,3,2:T(2,128)(2,1)}, bf16[2,128,12,64]{1,0,3,2:T(2,128)(2,1)S(1)}, u32[]{:S(2)}) copy-start(bf16[2,128,12,64]{1,0,3,2:T(2,128)(2,1)S(1)} %copy.93) | copy-start | bytes 1179652
  128.4 34.3 %copy-start.21 = (f32[256]{0:T(256)}, f32[256]{0:T(256)S(1)}, u32[]{:S(2)}) copy-start(f32[256]{0:T(256)S(1)} %broadcast_multiply_fusion.4) | copy-start | bytes 3076
  128.6 13.6 %copy-start.26 = (f32[256]{0:T(256)}, f32[256]{0:T(256)S(1)}, u32[]{:S(2)}) copy-start(f32[256]{0:T(256)S(1)} %add_rsqrt_fusion.1) | copy-start | bytes 3076
  142.2 7.4 %copy-start.2 = (bf16[2,1,128,768]{3,2,1,0:T(8,128)(2,1)S(1)}, bf16[2,1,128,768]{3,2,1,0:T(8,128)(2,1)}, u32[]{:S(2)}) copy-start(bf16[2,1,128,768]{3,2,1,0:T(8,128)(2,1)} %param.29) | copy-start | bytes 1179652
  146.5 0.8 copy-start.23
  149.5 4.5 %copy-start.29 = (f32[256,3072]{1,0:T(8,128)S(1)}, f32[256,3072]{1,0:T(8,128)}, u32[]{:S(2)}) copy-start(f32[256,3072]{1,0:T(8,128)} %get-tuple-element.107) | copy-start | bytes 9437188
  152.1 8.3 %slice-start = ((s8[4718592]{0:T(1024)(128)(4,1)}), s8[4194304]{0:T(1024)(128)(4,1)S(1)}, s32[]{:S(2)}) async-start(s8[4718592]{0:T(1024)(128)(4,1)} %bitcast.179), calls=%async_computation | async-start | bytes 8388608
  154.0 6.4 %copy-start.9 = (f32[256,768]{1,0:T(8,128)}, f32[256,768]{1,0:T(8,128)S(1)}, u32[]{:S(2)}) copy-start(f32[256,768]{1,0:T(8,128)S(1)} %get-tuple-element.103) | copy-start | bytes 2359300
  154.0 6.4 %copy-start.27 = (f32[256]{0:T(256)S(1)}, f32[256]{0:T(256)}, u32[]{:S(2)}) copy-start(f32[256]{0:T(256)} %copy-done.26) | copy-start | bytes 3076
  154.0 6.4 %slice-start.1 = ((s8[4718592]{0:T(1024)(128)(4,1)}), s8[524288]{0:T(1024)(128)(4,1)S(1)}, s32[]{:S(2)}) async-start(s8[4718592]{0:T(1024)(128)(4,1)} %bitcast.179), calls=%async_computation.1 | async-start | bytes 1048576
  160.4 2.3 copy-start.16
  160.4 3.1 copy-start.18
  168.6 5.1 %copy-start.25 = (f32[2,12,128]{2,1,0:T(8,128)S(1)}, f32[2,12,128]{2,1,0:T(8,128)}, u32[]{:S(2)}) copy-start(f32[2,12,128]{2,1,0:T(8,128)} %copy-done.24) | copy-start | bytes 36868
  178.7 3.3 copy-start.5
  179.1 2.8 copy-start.8
  194.1 7.0 %copy-start.11 = (f32[256,768]{1,0:T(8,128)S(1)}, f32[256,768]{1,0:T(8,128)}, u32[]{:S(2)}) copy-start(f32[256,768]{1,0:T(8,128)} %convolution_add_fusion.1) | copy-start | bytes 2359300
  203.2 18.1 %copy-start.1 = (bf16[4,2,128,768]{3,2,0,1:T(8,128)(2,1)S(1)}, bf16[4,2,128,768]{3,2,0,1:T(8,128)(2,1)}, u32[]{:S(2)}) copy-start(bf16[4,2,128,768]{3,2,0,1:T(8,128)(2,1)} %copy-done) | copy-start | bytes 4718596
  223.2 5.1 %copy-start.3 = (bf16[768,768]{0,1:T(8,128)(2,1)S(1)}, bf16[768,768]{0,1:T(8,128)(2,1)}, u32[]{:S(2)}) copy-start(bf16[768,768]{0,1:T(8,128)(2,1)} %convolution_convert_fusion.4) | copy-start | bytes 3538948
  228.3 2.1 copy-start.14
  228.3 3.6 %copy-start.17 = (bf16[256,3072]{1,0:T(8,128)(2,1)S(1)}, bf16[256,3072]{1,0:T(8,128)(2,1)}, u32[]{:S(2)}) copy-start(bf16[256,3072]{1,0:T(8,128)(2,1)} %copy-done.16) | copy-start | bytes 4718596
  228.3 3.6 %copy-start.22 = (f32[256]{0:T(256)S(1)}, f32[256]{0:T(256)}, u32[]{:S(2)}) copy-start(f32[256]{0:T(256)} %copy-done.21) | copy-start | bytes 3076
  228.3 3.6 %copy-start.28 = (f32[256]{0:T(256)S(1)}, f32[256]{0:T(256)}, u32[]{:S(2)}) copy-start(f32[256]{0:T(256)} %copy-done.26) | copy-start | bytes 3076
  231.9 3.7 %copy-start.6 = (bf16[256,3072]{1,0:T(8,128)(2,1)S(1)}, bf16[256,3072]{1,0:T(8,128)(2,1)}, u32[]{:S(2)}) copy-start(bf16[256,3072]{1,0:T(8,128)(2,1)} %get-tuple-element.106) | copy-start | bytes 4718596
  231.9 3.7 %copy-start.10 = (f32[256,768]{1,0:T(8,128)S(1)}, f32[256,768]{1,0:T(8,128)}, u32[]{:S(2)}) copy-start(f32[256,768]{1,0:T(8,128)} %copy-done.9) | copy-start | bytes 2359300

commit v2 on v0

--- a/solution.py
+++ b/solution.py
@@ -1,8 +1,11 @@
+import functools
 import math
 
 import jax
 import jax.numpy as jnp
 from jax import lax
+from jax.experimental import pallas as pl
+from jax.experimental.pallas import tpu as pltpu
 from jax.sharding import PartitionSpec as P
 
 HEADS = 12
@@ -364,9 +367,707 @@
     )
 
 
+MESH = pl.DeviceIdType.MESH
+ZS, CS, YS, XS = 4, 2, 2, 2
+def place():
+    dp = lax.axis_index("dp"); seq = lax.axis_index("seq")
+    return dp // CS, dp % CS, seq // XS, seq % XS
+def dev(z, c, y, x):
+    return (z * CS + c, y * XS + x)
+def greet(z, c, y, x):
+    barrier = pltpu.get_barrier_semaphore()
+    partners = [dev((z + k) % ZS, c, y, x) for k in (1, 2, 3)]
+    partners += [dev(z, 1 - c, y, x), dev(z, c, 1 - y, x), dev(z, c, y, 1 - x)]
+    for p in partners:
+        pl.semaphore_signal(barrier, inc=1, device_id=p, device_id_type=MESH)
+    pl.semaphore_wait(barrier, len(partners))
+def block(ref, r, z, c, y, x, *cols):
+    at = pl.multiple_of((((z * CS + c) * YS + y) * XS + x) * r, 8)
+    return ref.at[(pl.ds(at, r),) + cols]
+
+
+def gather_tasks(ins, tok, outs, tout, sems):
+    n = len(ins)
+    (loc, zs, zr, xs, xr, ys, yr, as_, ar, bs, br, cs, cr, ts, tr) = sems
+    z, c, y, x = place()
+    X, Y = 1 - x, 1 - y
+    xn, yn, cn = dev(z, c, y, X), dev(z, c, Y, x), dev(z, 1 - c, y, x)
+
+    def rc(src, dst, s, r, d):
+        return pltpu.make_async_remote_copy(src_ref=src, dst_ref=dst, send_sem=s, recv_sem=r, device_id=d, device_id_type=MESH)
+
+    sent, local = [], []
+
+    def go(cp):
+        cp.start()
+        sent.append(cp)
+
+    hh = tok.shape[-1] // 2
+
+    def begin():
+        greet(z, c, y, x)
+        for w in range(n + 1):
+            pair = (ins[w], block(outs[w], ins[w].shape[0], z, c, y, x)) if w < n else (tok, tout.at[y, x])
+            cp = pltpu.make_async_copy(*pair, loc.at[w])
+            cp.start()
+            local.append(cp)
+        for w in range(n):
+            o = block(outs[w], ins[w].shape[0], z, c, y, x)
+            for k in (1, 2, 3):
+                go(rc(ins[w], o, zs.at[w, k - 1], zr.at[w, k - 1], dev((z + k) % ZS, c, y, x)))
+            go(rc(ins[w], o, xs.at[w, 0], xr.at[w, 0], xn))
+            go(rc(ins[w], o, ys.at[w, 0], yr.at[w, 0], yn))
+            go(rc(ins[w], o, cs.at[w, 0, 0], cr.at[w, 0, 0], cn))
+            if w == 1:
+                to = tout.at[y, x]
+                go(rc(tok, to, ts.at[0], tr.at[0], xn))
+                go(rc(tok, to, ts.at[1], tr.at[1], yn))
+
+    def line(w, k):
+        o = block(outs[w], ins[w].shape[0], (z + ZS - k) % ZS, c, y, x)
+        rc(o, o, zs.at[w, k - 1], zr.at[w, k - 1], xn).wait_recv()
+        go(rc(o, o, xs.at[w, k], xr.at[w, k], xn))
+        go(rc(o, o, ys.at[w, k], yr.at[w, k], yn))
+        go(rc(o, o, cs.at[w, k, 0], cr.at[w, k, 0], cn))
+
+    def relay(w, k):
+        q = (z + ZS - k) % ZS
+        bx, by = block(outs[w], ins[w].shape[0], q, c, y, X), block(outs[w], ins[w].shape[0], q, c, Y, x)
+        h = ins[w].shape[-1] // 2
+        rc(bx, bx, xs.at[w, k], xr.at[w, k], xn).wait_recv()
+        a = block(outs[w], ins[w].shape[0], q, c, y, X, pl.ds(0, h))
+        go(rc(a, a, as_.at[w, k], ar.at[w, k], yn))
+        go(rc(bx, bx, cs.at[w, k, 1], cr.at[w, k, 1], cn))
+        rc(by, by, ys.at[w, k], yr.at[w, k], yn).wait_recv()
+        b = block(outs[w], ins[w].shape[0], q, c, Y, x, pl.ds(h, h))
+        go(rc(b, b, bs.at[w, k], br.at[w, k], xn))
+        go(rc(by, by, cs.at[w, k, 2], cr.at[w, k, 2], cn))
+
+    def corner(w, k):
+        h = ins[w].shape[-1] // 2
+        q = (z + ZS - k) % ZS
+        d = block(outs[w], ins[w].shape[0], q, c, Y, X)
+        a = block(outs[w], ins[w].shape[0], q, c, Y, X, pl.ds(0, h))
+        b = block(outs[w], ins[w].shape[0], q, c, Y, X, pl.ds(h, h))
+        rc(a, a, as_.at[w, k], ar.at[w, k], yn).wait_recv()
+        rc(b, b, bs.at[w, k], br.at[w, k], xn).wait_recv()
+        go(rc(d, d, cs.at[w, k, 3], cr.at[w, k, 3], cn))
+
+    def arrive(w, k):
+        q = (z + ZS - k) % ZS
+        for j, (yy, xx) in enumerate(((y, x), (y, X), (Y, x), (Y, X))):
+            o = block(outs[w], ins[w].shape[0], q, 1 - c, yy, xx)
+            rc(o, o, cs.at[w, k, j], cr.at[w, k, j], cn).wait_recv()
+
+    def own(w):
+        local[w].wait()
+
+    def tok_relay():
+        bx, by = tout.at[y, X], tout.at[Y, x]
+        rc(bx, bx, ts.at[0], tr.at[0], xn).wait_recv()
+        a = tout.at[y, X, :, :, pl.ds(0, hh)]
+        go(rc(a, a, ts.at[2], tr.at[2], yn))
+        rc(by, by, ts.at[1], tr.at[1], yn).wait_recv()
+        b = tout.at[Y, x, :, :, pl.ds(hh, hh)]
+        go(rc(b, b, ts.at[3], tr.at[3], xn))
+
+    def tok_corner():
+        a = tout.at[Y, X, :, :, pl.ds(0, hh)]
+        b = tout.at[Y, X, :, :, pl.ds(hh, hh)]
+        rc(a, a, ts.at[2], tr.at[2], yn).wait_recv()
+        rc(b, b, ts.at[3], tr.at[3], xn).wait_recv()
+        local[n].wait()
+
+    def finish():
+        for cp in sent:
+            cp.wait_send()
+
+    P = functools.partial
+    tasks = {"start": [begin], "end": [finish]}
+    K = range(ZS)
+
+    def lines(w): return [P(line, w, k) for k in K if k]
+    def relays(w): return [P(relay, w, k) for k in K]
+    def ends(w): return [P(corner, w, k) for k in K]
+    def last(w): return [P(arrive, w, k) for k in K] + [P(own, w)]
+
+    tasks[0] = lines(0) + lines(1) + relays(0) + relays(1) + [tok_relay] + lines(2) + lines(3) + ends(0) + ends(1)
+    tasks[1] = lines(4) + relays(2) + last(0) + last(1)
+    tasks[(2, 0)] = [tok_corner] + relays(3)[:2]
+    tasks[(2, 1)] = relays(3)[2:] + ends(2)
+    tasks[(2, 2)] = relays(4)[:1] + last(2)
+    tasks[(3, 0)] = relays(4)[1:2] + ends(3)[:1]
+    tasks[(3, 1)] = relays(4)[2:3] + ends(3)[1:2]
+    tasks[(3, 2)] = relays(4)[3:] + ends(3)[2:]
+    tasks[(3, 3)] = ends(4)[:2] + last(3)
+    tasks[4] = ends(4)[2:] + last(4)
+    return tasks
+
+
+F32, BF16 = jnp.float32, jnp.bfloat16
+LANE = 128
+
+
+def nt(a, b):
+    return lax.dot_general(a, b, (((1,), (1,)), ((), ())), preferred_element_type=F32)
+
+
+def tn(a, b):
+    return lax.dot_general(a, b, (((0,), (0,)), ((), ())), preferred_element_type=F32)
+
+
+def chunks(total, size, body):
+    def one(i, _):
+        body(pl.ds(pl.multiple_of(i * size, size), size))
+        return 0
+
+    lax.fori_loop(0, total // size, one, 0)
+
+
+def spread(width, per, owners_count):
+    n = lax.broadcasted_iota(jnp.int32, (1, width), 1)
+    block = jnp.floor((n.astype(F32) + 0.5) / per).astype(jnp.int32)
+    pick = lax.broadcasted_iota(jnp.int32, (LANE, width), 0) == n - block * per
+    mine = lax.broadcasted_iota(jnp.int32, (owners_count, width), 0) == block
+    return pick.astype(F32), mine.astype(F32)
+
+
+def split_heads(v):
+    low = lax.broadcasted_iota(jnp.int32, v.shape, 1) < v.shape[1] // 2
+    return jnp.concatenate([jnp.where(low, v, 0.0), jnp.where(low, 0.0, v)], axis=0).astype(BF16)
+
+
+def join_heads(v):
+    half = v.shape[0] // 2
+    low = lax.broadcasted_iota(jnp.int32, (half, v.shape[1]), 1) < v.shape[1] // 2
+    return jnp.where(low, v[:half], v[half:])
+
+
+def front_body(widths, *refs):
+    (svec, sqkv, sout, sup, sdown, tok, cot, starts) = refs[:8]
+    (gvec, gqkv, gout, gup, gdown, tout, lout, probs, qs, kv, att, normed1, inv1, inner, act, gp, dres2, rows, sums) = refs[8:27]
+    (wqkv, wout, wup, wdown, vecs, bias, mixed, wsem) = refs[27:35]
+    comm = refs[35:]
+    micro, nrow, width = tok.shape
+    count = micro * nrow
+    length = nrow * YS * XS
+    ff = sup.shape[1]
+    ins = (svec, sqkv, sout, sup, sdown)
+    outs = (gvec, gqkv, gout, gup, gdown)
+    tasks = gather_tasks(ins, tok, outs, tout, comm)
+    run = lambda name: [f() for f in tasks[name]]
+    run("start")
+    lin = [(gvec, vecs), (gqkv, wqkv), (gout, wout), (gup, wup), (gdown, wdown)]
+
+    def fetch(w):
+        src, dst = lin[w]
+        cp = pltpu.make_async_copy(src.reshape(dst.shape) if w == 0 else src, dst, wsem.at[w])
+        cp.start()
+        return cp
+
+    seq = lax.axis_index("seq")
+    qpos = seq * nrow + lax.broadcasted_iota(jnp.int32, (nrow, length), 0)
+    kpos = lax.broadcasted_iota(jnp.int32, (nrow, length), 1)
+    for m in range(micro):
+        ok = kpos <= qpos
+        for j in range(starts.shape[1]):
+            s = starts[m, j]
+            both = (qpos >= s) & (qpos < s + PIC) & (kpos >= s) & (kpos < s + PIC)
+            ok = ok | both
+        bias[m] = jnp.where(ok, 0.0, NEG)
+    run(0)
+    run(1)
+    first = [fetch(0), fetch(1)]
+    for cp in first:
+        cp.wait()
+    nown = vecs.shape[0]
+    made = {}
+    for r, n in enumerate(widths):
+        if n not in made:
+            made[n] = spread(n * nown, n, nown)
+        pick, mine = made[n]
+        got = jnp.dot(vecs[:, r, 0:LANE], pick, preferred_element_type=F32)
+        rows[r : r + 1, 0 : n * nown] = jnp.sum(got * mine, axis=0, keepdims=True)
+    src = tok[...].reshape(count, width)
+    head_scale = 1.0 / math.sqrt(width // HEADS)
+
+    def make_q(at):
+        qs[:, at] = (jnp.dot(tok[...].reshape(count, width), wqkv[:, at], preferred_element_type=F32) + rows[0:1, at]).astype(BF16)
+
+    chunks(width, 384, make_q)
+    run((2, 0))
+    for m in range(micro):
+        whole = tout[:, :, m].reshape(length, width)
+
+        def make_k(i, _):
+            at = pl.ds(pl.multiple_of(width + i * 384, 128), 384)
+            to = pl.ds(pl.multiple_of(i * 384, 128), 384)
+            kv[m, :, to] = jnp.dot(whole, wqkv[:, at], preferred_element_type=F32).astype(BF16)
+            return 0
+
+        def make_v(i, _):
+            at = pl.ds(pl.multiple_of(2 * width + i * 384, 128), 384)
+            to = pl.ds(pl.multiple_of(width + i * 384, 128), 384)
+            kv[m, :, to] = (jnp.dot(whole, wqkv[:, at], preferred_element_type=F32) + rows[0:1, to]).astype(BF16)
+            return 0
+
+        lax.fori_loop(0, width // 384, make_k, 0)
+        lax.fori_loop(0, width // 384, make_v, 0)
+        run((2, 1 + m))
+    pairs = width // LANE
+    for m in range(micro):
+        both = jnp.concatenate([bias[m], bias[m]], axis=0)
+
+        def attend(p, _):
+            at = pl.ds(pl.multiple_of(p * LANE, LANE), LANE)
+            vat = pl.ds(pl.multiple_of(width + p * LANE, LANE), LANE)
+            q2 = split_heads(qs[m * nrow : (m + 1) * nrow, at].astype(F32) * head_scale)
+            score = nt(q2, kv[m, :, at]) + jnp.concatenate([bias[m], bias[m]], axis=0)
+            expo = jnp.exp(score - jnp.max(score, axis=1, keepdims=True))
+            low = (expo * (1.0 / jnp.sum(expo, axis=1, keepdims=True))).astype(BF16)
+            probs[m * pairs + p] = low
+            o = join_heads(jnp.dot(low, kv[m, :, vat], preferred_element_type=F32))
+            att[m * nrow : (m + 1) * nrow, at] = o.astype(BF16)
+            return 0
+
+        for part in range(2):
+            lax.fori_loop(part * pairs // 2, (part + 1) * pairs // 2, attend, 0)
+            run((3, 2 * m + part))
+    cp = [fetch(2), fetch(3)]
+    cp[0].wait()
+
+    def project(at):
+        normed1[:, at] = tok[:, :, at].reshape(count, 384).astype(F32) + jnp.dot(att[...], wout[:, at], preferred_element_type=F32) + rows[1:2, at]
+
+    chunks(width, 384, project)
+    res = normed1[...]
+    centre = res - jnp.mean(res, axis=1, keepdims=True)
+    inverse = lax.rsqrt(jnp.mean(centre * centre, axis=1, keepdims=True) + EPS)
+    norm = centre * inverse
+    normed1[...] = norm
+    inv1[...] = jnp.broadcast_to(inverse, inv1.shape)
+    mix = norm * rows[2:3, 0:width] + rows[3:4, 0:width]
+    mixed[...] = mix
+    inner[...] = mix.astype(BF16)
+    cp[1].wait()
+
+    def feed(at):
+        pre = jnp.dot(inner[...], wup[:, at], preferred_element_type=F32) + rows[4:5, at]
+        cdf = 0.5 * (1.0 + lax.erf(pre * math.sqrt(0.5)))
+        act[:, at] = (pre * cdf).astype(BF16)
+        gp[:, at] = (cdf + pre * jnp.exp(-0.5 * pre * pre) * (1.0 / math.sqrt(2.0 * math.pi))).astype(BF16)
+
+    chunks(ff, 512, feed)
+    run(4)
+    last = fetch(4)
+    last.wait()
+
+    def out2(at):
+        dres2[:, at] = mixed[:, at] + jnp.dot(act[...], wdown[:, at], preferred_element_type=F32) + rows[5:6, at]
+
+    chunks(width, 256, out2)
+    res = dres2[...]
+    centre = res - jnp.mean(res, axis=1, keepdims=True)
+    inverse = lax.rsqrt(jnp.mean(centre * centre, axis=1, keepdims=True) + EPS)
+    norm = centre * inverse
+    gain = rows[6:7, 0:width]
+    lout[...] = (norm * gain + rows[7:8, 0:width]).astype(BF16)
+    up = cot[...].astype(F32)
+    scaled = up * gain
+    dres = inverse * (scaled - jnp.mean(scaled, axis=1, keepdims=True) - norm * jnp.mean(scaled * norm, axis=1, keepdims=True))
+    dres2[...] = dres
+    sums[0:1] = jnp.sum(dres.astype(BF16).astype(F32), axis=0, keepdims=True)
+    sums[1:2] = jnp.sum(up * norm, axis=0, keepdims=True)
+    sums[2:3] = jnp.sum(up, axis=0, keepdims=True)
+    run("end")
+
+
+def front(shards, tok, cot, starts, widths):
+    n = len(shards)
+    D, V, ANY = pltpu.SemaphoreType.DMA, pltpu.VMEM, pl.ANY
+    micro, nrow, width = tok.shape
+    count, length, ff = micro * nrow, nrow * YS * XS, shards[3].shape[1]
+    pairs = micro * width // LANE
+    S = jax.ShapeDtypeStruct
+    outs = [S((ZS * CS * YS * XS * s.shape[0], s.shape[1]), s.dtype) for s in shards]
+    vm = [
+        S((YS, XS) + tok.shape, BF16), S((count, width), BF16), S((pairs, 2 * nrow, length), BF16),
+        S((count, width), BF16), S((micro, length, 2 * width), BF16), S((count, width), BF16),
+        S((count, width), F32), S((count, LANE), F32), S((count, width), BF16), S((count, ff), BF16),
+        S((count, ff), BF16), S((count, width), F32), S((8, ff), F32), S((8, width), F32),
+    ]
+    total = ZS * CS * YS * XS
+    scr = [V((total * s.shape[0], s.shape[1]), BF16) for s in shards[1:]]
+    scr += [V((total,) + shards[0].shape, F32), V((micro, nrow, length), F32), V((count, width), F32), D((n,))]
+    scr += [D((n + 1,)), D((n, 3)), D((n, 3))] + [D((n, 4))] * 8 + [D((n, 4, 4))] * 2 + [D((4,))] * 2
+    return pl.pallas_call(
+        functools.partial(front_body, widths),
+        out_shape=outs + vm,
+        in_specs=[pl.BlockSpec(memory_space=V)] * (n + 2) + [pl.BlockSpec(memory_space=pltpu.SMEM)],
+        out_specs=[pl.BlockSpec(memory_space=ANY)] * n + [pl.BlockSpec(memory_space=V)] * len(vm),
+        scratch_shapes=scr,
+        compiler_params=pltpu.CompilerParams(collective_id=0, has_side_effects=True, vmem_limit_bytes=63 * 2**20),
+        name="front",
+    )(*shards, tok, cot, starts)
+
+
+def scatter_tasks(gs, stage, tparts, outs, tout, hold, sems):
+    n = len(gs)
+    hs, rbs, ras, rys, r2as, r2bs, rzs = (hold[i * n : (i + 1) * n] for i in range(7))
+    tx, ty, t2a, t2b, base = hold[7 * n :]
+    loc, wr, ss, sr, tss, tsr, cs, cr = sems
+    z, c, y, x = place()
+    X, Y = 1 - x, 1 - y
+    xn, yn, cn = dev(z, c, y, X), dev(z, c, Y, x), dev(z, 1 - c, y, x)
+
+    def rc(src, dst, s, r, d):
+        return pltpu.make_async_remote_copy(src_ref=src, dst_ref=dst, send_sem=s, recv_sem=r, device_id=d, device_id_type=MESH)
+
+    sent = []
+
+    def go(cp):
+        cp.start()
+        sent.append(cp)
+
+    A = [pl.ds(0, h.shape[-1] // 2) for h in hs]
+    B = [pl.ds(h.shape[-1] // 2, h.shape[-1] // 2) for h in hs]
+    hh = tparts.shape[-1] // 2
+    TA, TB = pl.ds(0, hh), pl.ds(hh, hh)
+
+    def write(w):
+        return pltpu.make_async_copy(stage[w], gs[w].reshape(stage[w].shape) if w == n - 1 else gs[w], wr.at[w])
+
+    spots = [(i, yy, xx) for i in range(ZS) for yy in range(YS) for xx in range(XS)]
+
+    def load(w, k):
+        i, yy, xx = spots[k]
+        return pltpu.make_async_copy(block(gs[w], hs[w].shape[3], i, c, yy, xx), hs[w].at[i, yy, xx], loc.at[w, k])
+
+    def swap(w, k):
+        i, yy, xx = spots[k]
+        return rc(block(gs[w], hs[w].shape[3], i, 1 - c, yy, xx), rbs[w].at[i, yy, xx], cs.at[w, k], cr.at[w, k], cn)
+
+    def s1a(w): return rc(hs[w].at[:, :, X, :, A[w]], ras[w], ss.at[w, 1], sr.at[w, 1], xn)
+    def s1b(w): return rc(hs[w].at[:, Y, :, :, B[w]], rys[w], ss.at[w, 2], sr.at[w, 2], yn)
+    def s2a(w): return rc(hs[w].at[:, Y, x, :, A[w]], r2as[w], ss.at[w, 3], sr.at[w, 3], yn)
+    def s2b(w): return rc(hs[w].at[:, y, X, :, B[w]], r2bs[w], ss.at[w, 4], sr.at[w, 4], xn)
+    def s3(w, k): return rc(hs[w].at[(z + k) % ZS, y, x], rzs[w].at[k - 1], ss.at[w, 4 + k], sr.at[w, 4 + k], dev((z + k) % ZS, c, y, x))
+
+    def put(w):
+        write(w).start()
+
+    def post(w):
+        write(w).wait()
+        for k in range(len(spots)):
+            load(w, k).start()
+            go(swap(w, k))
+
+    def plus(a, b, t):
+        return (a.astype(F32) + b.astype(F32)).astype(t)
+
+    def st0(w):
+        for k in range(len(spots)):
+            load(w, k).wait()
+            swap(w, k).wait_recv()
+
+        def one(i, _):
+            for yy in range(YS):
+                for xx in range(XS):
+                    hs[w][i, yy, xx] = plus(hs[w][i, yy, xx], rbs[w][i, yy, xx], hs[w].dtype)
+            return 0
+
+        lax.fori_loop(0, ZS, one, 0)
+        go(s1a(w))
+        go(s1b(w))
+
+    def st1(w):
+        s1a(w).wait_recv()
+        s1b(w).wait_recv()
+
+        def one(i, _):
+            for j in range(2):
+                hs[w][i, j, x, :, A[w]] = plus(hs[w][i, j, x, :, A[w]], ras[w][i, j], hs[w].dtype)
+                hs[w][i, y, j, :, B[w]] = plus(hs[w][i, y, j, :, B[w]], rys[w][i, j], hs[w].dtype)
+            return 0
+
+        lax.fori_loop(0, ZS, one, 0)
+        go(s2a(w))
+        go(s2b(w))
+
+    def st2(w):
+        s2a(w).wait_recv()
+        s2b(w).wait_recv()
+
+        def one(i, _):
+            hs[w][i, y, x, :, A[w]] = plus(hs[w][i, y, x, :, A[w]], r2as[w][i], hs[w].dtype)
+            hs[w][i, y, x, :, B[w]] = plus(hs[w][i, y, x, :, B[w]], r2bs[w][i], hs[w].dtype)
+            return 0
+
+        lax.fori_loop(0, ZS, one, 0)
+        for k in (1, 2, 3):
+            go(s3(w, k))
+
+    def st3(w):
+        total = hs[w][z, y, x].astype(F32)
+        for k in (1, 2, 3):
+            s3(w, k).wait_recv()
+            total = total + rzs[w][k - 1].astype(F32)
+        outs[w][...] = total
+
+    def t0():
+        go(rc(tparts.at[:, X, :, :, TA], tx, tss.at[0], tsr.at[0], xn))
+        go(rc(tparts.at[Y, :, :, :, TB], ty, tss.at[1], tsr.at[1], yn))
+
+    def t1():
+        rc(tx, tx, tss.at[0], tsr.at[0], xn).wait_recv()
+        rc(ty, ty, tss.at[1], tsr.at[1], yn).wait_recv()
+        tparts[Y, x, :, :, TA] = plus(tparts[Y, x, :, :, TA], tx[Y], BF16)
+        tparts[y, X, :, :, TB] = plus(tparts[y, X, :, :, TB], ty[X], BF16)
+        go(rc(tparts.at[Y, x, :, :, TA], t2a, tss.at[2], tsr.at[2], yn))
+        go(rc(tparts.at[y, X, :, :, TB], t2b, tss.at[3], tsr.at[3], xn))
+
+    def t2():
+        rc(t2a, t2a, tss.at[2], tsr.at[2], yn).wait_recv()
+        rc(t2b, t2b, tss.at[3], tsr.at[3], xn).wait_recv()
+        own = base[...].reshape(tout.shape) + tparts[y, x].astype(F32)
+        low = jnp.concatenate([tx[y].astype(F32) + t2a[...].astype(F32), ty[x].astype(F32) + t2b[...].astype(F32)], axis=2)
+        tout[...] = own + low
+
+    def done():
+        for cp in sent:
+            cp.wait_send()
+
+    return lambda: greet(z, c, y, x), put, post, (st0, st1, st2, st3), (t0, t1, t2), done
+
+
+def back_body(widths, *refs):
+    (wg, tok, probs, qs, kv, att, normed1, inv1, inner, act, gp, dres2, rows, sums) = (refs[0:4],) + refs[4:17]
+    k = 17
+    outs, tout, gs = refs[k : k + 5], refs[k + 5], refs[k + 6 : k + 11]
+    k += 11
+    wdown, wup, wout, wqkv, dpre, dkv, dq, datt, tpart, vscr = refs[k : k + 10]
+    k += 10
+    hold = refs[k : k + 40]
+    base = hold[39]
+    wsem, gsem = refs[k + 40 : k + 42]
+    sems = refs[k + 42 :]
+    micro, nrow, width = tok.shape[2:]
+    count, length = micro * nrow, nrow * YS * XS
+    ff = act.shape[1]
+    pairs = width // LANE
+    seq = lax.axis_index("seq")
+    stage = (wdown, wup, wout, wqkv, vscr)
+    begin, put, post, (st0, st1, st2, st3), (t0, t1, t2), done = scatter_tasks(gs, stage, tpart, outs, tout, hold, sems)
+    loads = [pltpu.make_async_copy(wg[i], stage[i], wsem.at[i]) for i in range(4)]
+    gload = pltpu.make_async_copy(gp, dpre, gsem.at[0])
+    gload.start()
+    for cp in loads:
+        cp.start()
+    begin()
+    head_scale = 1.0 / math.sqrt(width // HEADS)
+    vscr[...] = jnp.zeros(vscr.shape, F32)
+    nown = vscr.shape[0]
+
+    def vec(r, value):
+        n = widths[r]
+        pick, mine = spread(n * nown, n, nown)
+        vscr[:, r, 0:LANE] = lax.dot_general(value * mine, pick, (((1,), (1,)), ((), ())), precision=lax.Precision.HIGHEST, preferred_element_type=F32)
+
+    gload.wait()
+    loads[0].wait()
+    half = 512
+
+    def feed(at):
+        d = nt(dres2[...].astype(BF16), wdown[at, :])
+        dpre[:, at] = (d * dpre[:, at].astype(F32)).astype(BF16)
+
+    chunks(ff, half, feed)
+
+    def gdown(at):
+        wdown[at, :] = tn(act[:, at], dres2[...].astype(BF16)).astype(BF16)
+
+    chunks(ff, half, gdown)
+    put(0)
+    loads[1].wait()
+
+    def dmix(at):
+        base[:, at] = dres2[:, at] + nt(dpre[...], wup[at, :])
+
+    chunks(width, 256, dmix)
+    post(0)
+
+    def gup(at):
+        wup[:, at] = tn(inner[...], dpre[:, at]).astype(BF16)
+
+    chunks(ff, half, gup)
+    put(1)
+    dm, normed = base[...], normed1[...]
+    vec(2, jnp.sum(dm * normed, axis=0, keepdims=True))
+    vec(3, jnp.sum(dm, axis=0, keepdims=True))
+    scaled = dm * rows[2:3, 0:width]
+    d1 = inv1[:, 0:1] * (scaled - jnp.mean(scaled, axis=1, keepdims=True) - normed * jnp.mean(scaled * normed, axis=1, keepdims=True))
+    base[...] = d1
+    vec(1, jnp.sum(d1.astype(BF16).astype(F32), axis=0, keepdims=True))
+    post(1)
+    st0(0)
+    loads[2].wait()
+
+    def back_out(at):
+        datt[:, at] = nt(base[...].astype(BF16), wout[at, :]).astype(BF16)
+
+    chunks(width, 384, back_out)
+
+    def gout(at):
+        wout[:, at] = tn(att[...], base[:, at].astype(BF16)).astype(BF16)
+
+    chunks(width, 384, gout)
+    put(2)
+    pumps = [lambda: st0(1), lambda: (post(2), st1(0)), lambda: (st0(2), st1(1), st2(0)), lambda: (st1(2), st2(1))]
+    for m in range(micro):
+        mrow = slice(m * nrow, (m + 1) * nrow)
+
+        def attend(p, _):
+            at = pl.ds(pl.multiple_of(p * LANE, LANE), LANE)
+            vat = pl.ds(pl.multiple_of(width + p * LANE, LANE), LANE)
+            q2 = split_heads(qs[mrow, at].astype(F32) * head_scale)
+            o2 = split_heads(datt[mrow, at].astype(F32))
+            low = probs[m * pairs + p]
+            prob = low.astype(F32)
+            dprob = nt(o2, kv[m, :, vat])
+            delta = jnp.sum(prob * dprob, axis=1, keepdims=True)
+            ds = (prob * (dprob - delta)).astype(BF16)
+            dq[mrow, at] = (join_heads(jnp.dot(ds, kv[m, :, at], preferred_element_type=F32)) * head_scale).astype(BF16)
+            dkv[m, :, at] = tn(ds, q2).astype(BF16)
+            dkv[m, :, vat] = tn(low, o2).astype(BF16)
+            return 0
+
+        for part in range(2):
+            lax.fori_loop(part * pairs // 2, (part + 1) * pairs // 2, attend, 0)
+            pumps[2 * m + part]()
+    loads[3].wait()
+    for m in range(micro):
+
+        def piece(i, _):
+            at = pl.ds(pl.multiple_of(i * 256, 256), 256)
+            got = nt(dkv[m], wqkv[at, width : 3 * width])
+            tpart[:, :, m, :, at] = got.reshape(YS, XS, nrow, 256).astype(BF16)
+            return 0
+
+        lax.fori_loop(0, width // 256, piece, 0)
+    t0()
+
+    def dsrc(at):
+        base[:, at] = base[:, at] + nt(dq[...], wqkv[at, 0:width])
+
+    chunks(width, 256, dsrc)
+    st2(2)
+    src = tok.at[seq // XS, seq % XS]
+
+    def gq(at):
+        wqkv[:, at] = tn(src[...].reshape(count, width), dq[:, at]).astype(BF16)
+
+    chunks(width, 384, gq)
+
+    def gkv(i, _):
+        at = pl.ds(pl.multiple_of(i * 384, 128), 384)
+        to = pl.ds(pl.multiple_of(width + i * 384, 128), 384)
+        total = tn(tok[:, :, 0].reshape(length, width), dkv[0, :, at])
+        for m in range(1, micro):
+            total = total + tn(tok[:, :, m].reshape(length, width), dkv[m, :, at])
+        wqkv[:, to] = total.astype(BF16)
+        return 0
+
+    lax.fori_loop(0, 2 * width // 384, gkv, 0)
+    put(3)
+    dv = sum(jnp.sum(dkv[m, :, width:].astype(F32), axis=0, keepdims=True) for m in range(micro))
+    vec(0, jnp.concatenate([jnp.sum(dq[...].astype(F32), axis=0, keepdims=True), dv], axis=1))
+    vec(4, jnp.sum(dpre[...].astype(F32), axis=0, keepdims=True))
+    post(3)
+    for r in range(3):
+        vec(5 + r, sums[r : r + 1])
+    put(4)
+    st3(0)
+    post(4)
+    st0(3)
+    t1()
+    st3(1)
+    st0(4)
+    st3(2)
+    st1(3)
+    st1(4)
+    t2()
+    st2(3)
+    st2(4)
+    st3(3)
+    st3(4)
+    done()
+
+
+def back(weights, saved, widths):
+    D, V, ANY = pltpu.SemaphoreType.DMA, pltpu.VMEM, pl.ANY
+    S = jax.ShapeDtypeStruct
+    tok = saved[0]
+    total = ZS * CS * YS * XS
+    micro, nrow, width = tok.shape[2:]
+    count, length = micro * nrow, nrow * YS * XS
+    ff = saved[8].shape[1]
+    blocks = [(w.shape[0] // total, w.shape[1]) for w in weights] + [(8, 256)]
+    kinds = [BF16] * 4 + [F32]
+    both = list(zip(blocks, kinds))
+    outs = [S(b, F32) for b in blocks] + [S((micro, nrow, width), F32)]
+    outs += [S((total * b[0], b[1]), t) for b, t in both]
+    scr = [V((total * b[0], b[1]), BF16) for b in blocks[:4]]
+    scr += [V((count, ff), BF16), V((micro, length, 2 * width), BF16), V((count, width), BF16), V((count, width), BF16)]
+    scr += [V(tok.shape, BF16), V((total, 8, 256), F32)]
+    scr += [V((ZS, YS, XS) + b, t) for b, t in both] * 2
+    scr += [V((ZS, 2, b[0], b[1] // 2), t) for b, t in both] * 2
+    scr += [V((ZS, b[0], b[1] // 2), t) for b, t in both] * 2
+    scr += [V((ZS - 1,) + b, t) for b, t in both]
+    th = (micro, nrow, width // 2)
+    scr += [V((2,) + th, BF16)] * 2 + [V(th, BF16)] * 2 + [V((count, width), F32)]
+    scr += [D((4,)), D((1,)), D((5, 16)), D((5,)), D((5, 8)), D((5, 8)), D((4,)), D((4,)), D((5, 16)), D((5, 16))]
+    spec = lambda s: pl.BlockSpec(memory_space=s)
+    return pl.pallas_call(
+        functools.partial(back_body, widths),
+        out_shape=outs,
+        in_specs=[spec(ANY)] * 4 + [spec(V)] * 9 + [spec(ANY)] + [spec(V)] * 3,
+        out_specs=[spec(V)] * 6 + [spec(ANY)] * 5,
+        scratch_shapes=scr,
+        compiler_params=pltpu.CompilerParams(collective_id=1, has_side_effects=True, vmem_limit_bytes=67043328),
+        name="back",
+    )(*weights, *saved)
+
+
+def fits(mesh):
+    return mesh.shape["dp"] == ZS * CS and mesh.shape["seq"] == YS * XS
+
+
+def fast_device(
+    tokens, piece_starts, qkv_weight, qv_bias, out_weight, out_bias, norm1_gain, norm1_bias,
+    up_weight, up_bias, down_weight, down_bias, norm2_gain, norm2_bias, grad_out,
+):
+    micro, _, nrow, width = tokens.shape
+    small = (qv_bias, out_bias, norm1_gain, norm1_bias, up_bias, down_bias, norm2_gain, norm2_bias)
+    widths = tuple(v.shape[0] for v in small)
+    vector = jnp.stack([jnp.pad(v.astype(F32), (0, 256 - v.shape[0])) for v in small])
+    cot = grad_out.reshape(micro * nrow, width)
+    got = front(
+        (vector, qkv_weight, out_weight, up_weight, down_weight), tokens[:, 0], cot, piece_starts[:, 0], widths
+    )
+    gqkv, gout, gup, gdown = got[1:5]
+    layer_out = got[6]
+    shares = back((gdown, gup, gout, gqkv), (got[5],) + tuple(got[7:]), widths)
+    down, up, out, qkv, vec, tokens_grad = shares[:6]
+    v = [vec[r, :n] for r, n in enumerate(widths)]
+    return (
+        layer_out.reshape(tokens.shape), tokens_grad.reshape(tokens.shape),
+        qkv, v[0], out, v[1], v[2], v[3], up, v[4], down, v[5], v[6], v[7],
+    )
+
+
 def solution(mesh):
     return jax.shard_map(
-        on_device,
+        fast_device if fits(mesh) else on_device,
         mesh=mesh,
         in_specs=(
             P(None, "dp", "seq", None),

time: 934 us -> 237 us (0.25)
  waiting for transfers between devices: 608 us -> 0 us
  Pallas kernels: 0 us -> 218 us
  blocking collectives: 131 us -> 0 us
  matrix products: 86.2 us -> 0 us
  local copies, waits for them, and re-layouts: 57.5 us -> 17.7 us
  other arithmetic: 29.5 us -> 0.6 us
  between operations: 15.3 us -> 0.69 us
    reduce_scatter x3 -> x0, waiting for transfers between devices: 287 us -> none  [on_device(): lax.psum_scatter(totals, ('dp', 'seq'), scatter_dimension=0, tiled=True)]
    pallas_call x0 -> x2, Pallas kernels: none -> 218 us  [the longest x1 119 us: back(): pl.pallas_call(functools.partial(back_body, widths), out_shape=outs, in_s...]
    unnamed x17 -> x0, waiting for transfers between devices: 203 us -> none
    all_gather x4 -> x0, waiting for transfers between devices: 117 us -> none  [the longest x1 55.6 us: gather_forward(): lax.all_gather(shards[8], ('dp', 'seq'), axis=0, tiled=True)]
    dot_general x36 -> x0, matrix products: 86.2 us -> none  [the longest x8 24.8 us: matmul(): return jnp.dot(left, right, preferred_element_type=jnp.float32)]
    unnamed x2 -> x0, blocking collectives: 84.3 us -> none
    all_gather x4 -> x0, blocking collectives: 46.3 us -> none  [the longest x2 25.3 us: on_device(): key_piece = lax.all_gather(keys, 'seq', axis=0, tiled=True)]
    unnamed x177 -> x10, local copies, waits for them, and re-layouts: 46.3 us -> 8.42 us
  transfers between devices with their start and end apart: 12 -> 0, of which waited for: 10 -> 0; matrix products, arithmetic and copies ran while one was open for 14% -> 0% of each run, Pallas kernels for 0% -> 0%
where the time goes in v2:
time: 237 us
  Pallas kernels  218 us (92%)
  local copies, waits for them, and re-layouts  17.7 us (7%)
    pallas_call x1, Pallas kernels, back(): pl.pallas_call(functools.partial(back_body, widths), out_shape=outs, in_s...  119 us
    pallas_call x1, Pallas kernels, front(): pl.pallas_call(functools.partial(front_body, widths), out_shape=outs + vm...  98.9 us
    unnamed x10, local copies, waits for them, and re-layouts  8.42 us
    pad x8, local copies, waits for them, and re-layouts, fast_device(): jnp.pad(v.astype(F32), (0, 256 - v.shape[0]))  5.28 us

profile of v2, /device:TPU:0, one launch (start us, length us, event | category | flops | bytes accessed | tf_op | source)
XLA Modules:
  0.0 236.7 jit_solution(11083201299160569416)
XLA Ops:
  0.6 0.7 pad.35
  1.3 0.7 pad.36
  2.0 0.7 pad.37
  2.6 0.7 pad.38
  3.3 0.7 pad.39
  4.0 0.7 pad.40
  4.7 0.7 pad.41
  5.3 0.7 pad.42
  6.0 0.6 stack.46.refs_0_
  6.6 98.9 %front.1 = (f32[256,256]{1,0:T(8,128)}, bf16[768,2304]{1,0:T(8,128)(2,1)}, bf16[768,768]{1,0:T(8,128)(2,1)}, bf16[768,3072]{1,0:T(8,128)(2,1)}, bf16[3072,768]{1...) custom-call(f32[8,256]{1,0:T(8,128)} %stack.46.refs_0_, ...), custom_call_target="tpu_custom_call" | custom-call | tf_op jit(solution)/shard_map/front/pallas_call | solution.py:703
  105.5 118.9 %back.1 = (f32[96,768]{1,0:T(8,128)}, f32[24,3072]{1,0:T(8,128)}, f32[24,768]{1,0:T(8,128)}, f32[24,2304]{1,0:T(8,128)}, f32[8,256]{1,0:T(8,128)}, /*index=5*/f3...) custom-call(bf16[3072,768]{1,0:T(8,128)(2,1)} %get-tuple-element.39., ...), custom_call_target="tpu_custom_call" | custom-call | tf_op jit(solution)/shard_map/back/pallas_call | solution.py:1030
  224.4 0.0 copy-start.1
  224.4 0.0 copy-start
  224.4 1.3 slice_bitcast_fusion.3
  225.6 1.2 slice_bitcast_fusion.7
  226.8 1.4 slice_bitcast_fusion
  228.2 1.8 copy.37
  230.0 2.1 copy.38
  232.1 1.6 copy.39
  233.7 1.5 copy.40
  235.2 0.0 copy-done.1
  235.2 0.7 copy.41
  236.0 0.0 copy-done
  236.0 0.7 copy.42
  (9 shorter events, 0.1 us)
Async XLA Ops:
  224.4 10.9 %copy-start.1 = (f32[24,3072]{1,0:T(8,128)S(1)}, f32[24,3072]{1,0:T(8,128)}, u32[]{:S(2)}) copy-start(f32[24,3072]{1,0:T(8,128)} %get-tuple-element.104) | copy-start | bytes 884740
  224.4 11.6 %copy-start = (f32[96,768]{1,0:T(8,128)S(1)}, f32[96,768]{1,0:T(8,128)}, u32[]{:S(2)}) copy-start(f32[96,768]{1,0:T(8,128)} %get-tuple-element.106) | copy-start | bytes 884740

commit v3 on v2

--- a/solution.py
+++ b/solution.py
@@ -543,11 +543,156 @@
     return jnp.where(low, v[:half], v[half:])
 
 
-def front_body(widths, *refs):
-    (svec, sqkv, sout, sup, sdown, tok, cot, starts) = refs[:8]
-    (gvec, gqkv, gout, gup, gdown, tout, lout, probs, qs, kv, att, normed1, inv1, inner, act, gp, dres2, rows, sums) = refs[8:27]
-    (wqkv, wout, wup, wdown, vecs, bias, mixed, wsem) = refs[27:35]
-    comm = refs[35:]
+def scatter_tasks(gs, pieces, tparts, outs, tout, hold, sems):
+    n = len(pieces)
+    hs, rbs, ras, rys, r2as, r2bs, rzs = (hold[i * n : (i + 1) * n] for i in range(7))
+    tx, ty, t2a, t2b, base = hold[7 * n :]
+    loc, ss, sr, tss, tsr, cs, cr = sems
+    z, c, y, x = place()
+    X, Y = 1 - x, 1 - y
+    xn, yn, cn = dev(z, c, y, X), dev(z, c, Y, x), dev(z, 1 - c, y, x)
+
+    def rc(src, dst, s, r, d):
+        return pltpu.make_async_remote_copy(src_ref=src, dst_ref=dst, send_sem=s, recv_sem=r, device_id=d, device_id_type=MESH)
+
+    sent = []
+
+    def go(cp):
+        cp.start()
+        sent.append(cp)
+
+    A = [pl.ds(0, h.shape[-1] // 2) for h in hs]
+    B = [pl.ds(h.shape[-1] // 2, h.shape[-1] // 2) for h in hs]
+    hh = tparts.shape[-1] // 2
+    TA, TB = pl.ds(0, hh), pl.ds(hh, hh)
+
+    spots = [(i, yy, xx) for i in range(ZS) for yy in range(YS) for xx in range(XS)]
+
+    def load(w, k):
+        i, yy, xx = spots[k]
+        return pltpu.make_async_copy(block(gs[pieces[w][0]], hs[w].shape[3], i, c, yy, xx, pl.ds(*pieces[w][1:])), hs[w].at[i, yy, xx], loc.at[w, k])
+
+    def swap(w, k):
+        i, yy, xx = spots[k]
+        return rc(block(gs[pieces[w][0]], hs[w].shape[3], i, 1 - c, yy, xx, pl.ds(*pieces[w][1:])), rbs[w].at[i, yy, xx], cs.at[w, k], cr.at[w, k], cn)
+
+    def s1a(w): return rc(hs[w].at[:, :, X, :, A[w]], ras[w], ss.at[w, 1], sr.at[w, 1], xn)
+    def s1b(w): return rc(hs[w].at[:, Y, :, :, B[w]], rys[w], ss.at[w, 2], sr.at[w, 2], yn)
+    def s2a(w): return rc(hs[w].at[:, Y, x, :, A[w]], r2as[w], ss.at[w, 3], sr.at[w, 3], yn)
+    def s2b(w): return rc(hs[w].at[:, y, X, :, B[w]], r2bs[w], ss.at[w, 4], sr.at[w, 4], xn)
+    def s3(w, k): return rc(hs[w].at[(z + k) % ZS, y, x], rzs[w].at[k - 1], ss.at[w, 4 + k], sr.at[w, 4 + k], dev((z + k) % ZS, c, y, x))
+
+    def post(w):
+        for k in range(len(spots)):
+            load(w, k).start()
+            go(swap(w, k))
+
+    def plus(a, b, t):
+        return (a.astype(F32) + b.astype(F32)).astype(t)
+
+    def st0(w):
+        for k in range(len(spots)):
+            load(w, k).wait()
+            swap(w, k).wait_recv()
+
+        def one(i, _):
+            for yy in range(YS):
+                for xx in range(XS):
+                    hs[w][i, yy, xx] = plus(hs[w][i, yy, xx], rbs[w][i, yy, xx], hs[w].dtype)
+            return 0
+
+        lax.fori_loop(0, ZS, one, 0)
+        go(s1a(w))
+        go(s1b(w))
+
+    def st1(w):
+        s1a(w).wait_recv()
+        s1b(w).wait_recv()
+
+        def one(i, _):
+            for j in range(2):
+                hs[w][i, j, x, :, A[w]] = plus(hs[w][i, j, x, :, A[w]], ras[w][i, j], hs[w].dtype)
+                hs[w][i, y, j, :, B[w]] = plus(hs[w][i, y, j, :, B[w]], rys[w][i, j], hs[w].dtype)
+            return 0
+
+        lax.fori_loop(0, ZS, one, 0)
+        go(s2a(w))
+        go(s2b(w))
+
+    def st2(w):
+        s2a(w).wait_recv()
+        s2b(w).wait_recv()
+
+        def one(i, _):
+            hs[w][i, y, x, :, A[w]] = plus(hs[w][i, y, x, :, A[w]], r2as[w][i], hs[w].dtype)
+            hs[w][i, y, x, :, B[w]] = plus(hs[w][i, y, x, :, B[w]], r2bs[w][i], hs[w].dtype)
+            return 0
+
+        lax.fori_loop(0, ZS, one, 0)
+        for k in (1, 2, 3):
+            go(s3(w, k))
+
+    def st3(w):
+        total = hs[w][z, y, x].astype(F32)
+        for k in (1, 2, 3):
+            s3(w, k).wait_recv()
+            total = total + rzs[w][k - 1].astype(F32)
+        outs[pieces[w][0]][:, pl.ds(*pieces[w][1:])] = total
+
+    def t0():
+        go(rc(tparts.at[:, X, :, :, TA], tx, tss.at[0], tsr.at[0], xn))
+        go(rc(tparts.at[Y, :, :, :, TB], ty, tss.at[1], tsr.at[1], yn))
+
+    def t1():
+        rc(tx, tx, tss.at[0], tsr.at[0], xn).wait_recv()
+        rc(ty, ty, tss.at[1], tsr.at[1], yn).wait_recv()
+        tparts[Y, x, :, :, TA] = plus(tparts[Y, x, :, :, TA], tx[Y], BF16)
+        tparts[y, X, :, :, TB] = plus(tparts[y, X, :, :, TB], ty[X], BF16)
+        go(rc(tparts.at[Y, x, :, :, TA], t2a, tss.at[2], tsr.at[2], yn))
+        go(rc(tparts.at[y, X, :, :, TB], t2b, tss.at[3], tsr.at[3], xn))
+
+    def t2():
+        rc(t2a, t2a, tss.at[2], tsr.at[2], yn).wait_recv()
+        rc(t2b, t2b, tss.at[3], tsr.at[3], xn).wait_recv()
+        own = base[...].reshape(tout.shape) + tparts[y, x].astype(F32)
+        low = jnp.concatenate([tx[y].astype(F32) + t2a[...].astype(F32), ty[x].astype(F32) + t2b[...].astype(F32)], axis=2)
+        tout[...] = own + low
+
+    def done():
+        for cp in sent:
+            cp.wait_send()
+
+    return post, (st0, st1, st2, st3), (t0, t1, t2), done
+
+
+def mega_body(widths, pieces, *refs):
+    nv = len(widths)
+    small = refs[:nv]
+    (sqkv, sout, sup, sdown, tok, cot, starts) = refs[nv : nv + 7]
+    k = nv + 7
+    gweights = refs[k : k + 5]
+    gs = refs[k + 5 : k + 10]
+    lout = refs[k + 10]
+    shares, tgrad = refs[k + 11 : k + 16], refs[k + 16]
+    k += 17
+    (svec, tout, probs, qs, kv, att, normed1, inv1, inner, act, dpre, dres2, rows, sums) = refs[k : k + 14]
+    k += 14
+    (wqkv, wout, wup, wdown, vecs, bias, datt, dstage) = refs[k : k + 8]
+    k += 8
+    np_ = len(pieces)
+    hold = refs[k : k + 7 * np_ + 5]
+    base = hold[-1]
+    k += 7 * np_ + 5
+    wsem, psem, dsem = refs[k : k + 3]
+    comm = refs[k + 3 : k + 18]
+    sems = refs[k + 18 :]
+    gvec, gqkv, gout, gup, gdown = gweights
+    mixed, gp, vscr = base, dpre, vecs
+    spare = tok.shape[0] * tok.shape[1] * YS * XS
+    tpart = wdown.at[pl.ds(0, spare)].reshape((YS, XS) + tok.shape)
+    svec[...] = jnp.zeros(svec.shape, F32)
+    for r, v in enumerate(small):
+        svec[r : r + 1, 0 : widths[r]] = v[...].astype(F32)
     micro, nrow, width = tok.shape
     count = micro * nrow
     length = nrow * YS * XS
@@ -679,228 +824,62 @@
     sums[0:1] = jnp.sum(dres.astype(BF16).astype(F32), axis=0, keepdims=True)
     sums[1:2] = jnp.sum(up * norm, axis=0, keepdims=True)
     sums[2:3] = jnp.sum(up, axis=0, keepdims=True)
-    run("end")
-
-
-def front(shards, tok, cot, starts, widths):
-    n = len(shards)
-    D, V, ANY = pltpu.SemaphoreType.DMA, pltpu.VMEM, pl.ANY
-    micro, nrow, width = tok.shape
-    count, length, ff = micro * nrow, nrow * YS * XS, shards[3].shape[1]
-    pairs = micro * width // LANE
-    S = jax.ShapeDtypeStruct
-    outs = [S((ZS * CS * YS * XS * s.shape[0], s.shape[1]), s.dtype) for s in shards]
-    vm = [
-        S((YS, XS) + tok.shape, BF16), S((count, width), BF16), S((pairs, 2 * nrow, length), BF16),
-        S((count, width), BF16), S((micro, length, 2 * width), BF16), S((count, width), BF16),
-        S((count, width), F32), S((count, LANE), F32), S((count, width), BF16), S((count, ff), BF16),
-        S((count, ff), BF16), S((count, width), F32), S((8, ff), F32), S((8, width), F32),
-    ]
-    total = ZS * CS * YS * XS
-    scr = [V((total * s.shape[0], s.shape[1]), BF16) for s in shards[1:]]
-    scr += [V((total,) + shards[0].shape, F32), V((micro, nrow, length), F32), V((count, width), F32), D((n,))]
-    scr += [D((n + 1,)), D((n, 3)), D((n, 3))] + [D((n, 4))] * 8 + [D((n, 4, 4))] * 2 + [D((4,))] * 2
-    return pl.pallas_call(
-        functools.partial(front_body, widths),
-        out_shape=outs + vm,
-        in_specs=[pl.BlockSpec(memory_space=V)] * (n + 2) + [pl.BlockSpec(memory_space=pltpu.SMEM)],
-        out_specs=[pl.BlockSpec(memory_space=ANY)] * n + [pl.BlockSpec(memory_space=V)] * len(vm),
-        scratch_shapes=scr,
-        compiler_params=pltpu.CompilerParams(collective_id=0, has_side_effects=True, vmem_limit_bytes=63 * 2**20),
-        name="front",
-    )(*shards, tok, cot, starts)
-
-
-def scatter_tasks(gs, stage, tparts, outs, tout, hold, sems):
-    n = len(gs)
-    hs, rbs, ras, rys, r2as, r2bs, rzs = (hold[i * n : (i + 1) * n] for i in range(7))
-    tx, ty, t2a, t2b, base = hold[7 * n :]
-    loc, wr, ss, sr, tss, tsr, cs, cr = sems
-    z, c, y, x = place()
-    X, Y = 1 - x, 1 - y
-    xn, yn, cn = dev(z, c, y, X), dev(z, c, Y, x), dev(z, 1 - c, y, x)
-
-    def rc(src, dst, s, r, d):
-        return pltpu.make_async_remote_copy(src_ref=src, dst_ref=dst, send_sem=s, recv_sem=r, device_id=d, device_id_type=MESH)
-
-    sent = []
-
-    def go(cp):
-        cp.start()
-        sent.append(cp)
-
-    A = [pl.ds(0, h.shape[-1] // 2) for h in hs]
-    B = [pl.ds(h.shape[-1] // 2, h.shape[-1] // 2) for h in hs]
-    hh = tparts.shape[-1] // 2
-    TA, TB = pl.ds(0, hh), pl.ds(hh, hh)
-
-    def write(w):
-        return pltpu.make_async_copy(stage[w], gs[w].reshape(stage[w].shape) if w == n - 1 else gs[w], wr.at[w])
-
-    spots = [(i, yy, xx) for i in range(ZS) for yy in range(YS) for xx in range(XS)]
-
-    def load(w, k):
-        i, yy, xx = spots[k]
-        return pltpu.make_async_copy(block(gs[w], hs[w].shape[3], i, c, yy, xx), hs[w].at[i, yy, xx], loc.at[w, k])
-
-    def swap(w, k):
-        i, yy, xx = spots[k]
-        return rc(block(gs[w], hs[w].shape[3], i, 1 - c, yy, xx), rbs[w].at[i, yy, xx], cs.at[w, k], cr.at[w, k], cn)
-
-    def s1a(w): return rc(hs[w].at[:, :, X, :, A[w]], ras[w], ss.at[w, 1], sr.at[w, 1], xn)
-    def s1b(w): return rc(hs[w].at[:, Y, :, :, B[w]], rys[w], ss.at[w, 2], sr.at[w, 2], yn)
-    def s2a(w): return rc(hs[w].at[:, Y, x, :, A[w]], r2as[w], ss.at[w, 3], sr.at[w, 3], yn)
-    def s2b(w): return rc(hs[w].at[:, y, X, :, B[w]], r2bs[w], ss.at[w, 4], sr.at[w, 4], xn)
-    def s3(w, k): return rc(hs[w].at[(z + k) % ZS, y, x], rzs[w].at[k - 1], ss.at[w, 4 + k], sr.at[w, 4 + k], dev((z + k) % ZS, c, y, x))
-
-    def put(w):
-        write(w).start()
-
-    def post(w):
-        write(w).wait()
-        for k in range(len(spots)):
-            load(w, k).start()
-            go(swap(w, k))
-
-    def plus(a, b, t):
-        return (a.astype(F32) + b.astype(F32)).astype(t)
-
-    def st0(w):
-        for k in range(len(spots)):
-            load(w, k).wait()
-            swap(w, k).wait_recv()
-
-        def one(i, _):
-            for yy in range(YS):
-                for xx in range(XS):
-                    hs[w][i, yy, xx] = plus(hs[w][i, yy, xx], rbs[w][i, yy, xx], hs[w].dtype)
-            return 0
-
-        lax.fori_loop(0, ZS, one, 0)
-        go(s1a(w))
-        go(s1b(w))
-
-    def st1(w):
-        s1a(w).wait_recv()
-        s1b(w).wait_recv()
-
-        def one(i, _):
-            for j in range(2):
-                hs[w][i, j, x, :, A[w]] = plus(hs[w][i, j, x, :, A[w]], ras[w][i, j], hs[w].dtype)
-                hs[w][i, y, j, :, B[w]] = plus(hs[w][i, y, j, :, B[w]], rys[w][i, j], hs[w].dtype)
-            return 0
-
-        lax.fori_loop(0, ZS, one, 0)
-        go(s2a(w))
-        go(s2b(w))
-
-    def st2(w):
-        s2a(w).wait_recv()
-        s2b(w).wait_recv()
-
-        def one(i, _):
-            hs[w][i, y, x, :, A[w]] = plus(hs[w][i, y, x, :, A[w]], r2as[w][i], hs[w].dtype)
-            hs[w][i, y, x, :, B[w]] = plus(hs[w][i, y, x, :, B[w]], r2bs[w][i], hs[w].dtype)
-            return 0
-
-        lax.fori_loop(0, ZS, one, 0)
-        for k in (1, 2, 3):
-            go(s3(w, k))
-
-    def st3(w):
-        total = hs[w][z, y, x].astype(F32)
-        for k in (1, 2, 3):
-            s3(w, k).wait_recv()
-            total = total + rzs[w][k - 1].astype(F32)
-        outs[w][...] = total
-
-    def t0():
-        go(rc(tparts.at[:, X, :, :, TA], tx, tss.at[0], tsr.at[0], xn))
-        go(rc(tparts.at[Y, :, :, :, TB], ty, tss.at[1], tsr.at[1], yn))
-
-    def t1():
-        rc(tx, tx, tss.at[0], tsr.at[0], xn).wait_recv()
-        rc(ty, ty, tss.at[1], tsr.at[1], yn).wait_recv()
-        tparts[Y, x, :, :, TA] = plus(tparts[Y, x, :, :, TA], tx[Y], BF16)
-        tparts[y, X, :, :, TB] = plus(tparts[y, X, :, :, TB], ty[X], BF16)
-        go(rc(tparts.at[Y, x, :, :, TA], t2a, tss.at[2], tsr.at[2], yn))
-        go(rc(tparts.at[y, X, :, :, TB], t2b, tss.at[3], tsr.at[3], xn))
-
-    def t2():
-        rc(t2a, t2a, tss.at[2], tsr.at[2], yn).wait_recv()
-        rc(t2b, t2b, tss.at[3], tsr.at[3], xn).wait_recv()
-        own = base[...].reshape(tout.shape) + tparts[y, x].astype(F32)
-        low = jnp.concatenate([tx[y].astype(F32) + t2a[...].astype(F32), ty[x].astype(F32) + t2b[...].astype(F32)], axis=2)
-        tout[...] = own + low
-
-    def done():
-        for cp in sent:
-            cp.wait_send()
-
-    return lambda: greet(z, c, y, x), put, post, (st0, st1, st2, st3), (t0, t1, t2), done
-
-
-def back_body(widths, *refs):
-    (wg, tok, probs, qs, kv, att, normed1, inv1, inner, act, gp, dres2, rows, sums) = (refs[0:4],) + refs[4:17]
-    k = 17
-    outs, tout, gs = refs[k : k + 5], refs[k + 5], refs[k + 6 : k + 11]
-    k += 11
-    wdown, wup, wout, wqkv, dpre, dkv, dq, datt, tpart, vscr = refs[k : k + 10]
-    k += 10
-    hold = refs[k : k + 40]
-    base = hold[39]
-    wsem, gsem = refs[k + 40 : k + 42]
-    sems = refs[k + 42 :]
-    micro, nrow, width = tok.shape[2:]
-    count, length = micro * nrow, nrow * YS * XS
-    ff = act.shape[1]
     pairs = width // LANE
-    seq = lax.axis_index("seq")
-    stage = (wdown, wup, wout, wqkv, vscr)
-    begin, put, post, (st0, st1, st2, st3), (t0, t1, t2), done = scatter_tasks(gs, stage, tpart, outs, tout, hold, sems)
-    loads = [pltpu.make_async_copy(wg[i], stage[i], wsem.at[i]) for i in range(4)]
-    gload = pltpu.make_async_copy(gp, dpre, gsem.at[0])
-    gload.start()
-    for cp in loads:
-        cp.start()
-    begin()
-    head_scale = 1.0 / math.sqrt(width // HEADS)
     vscr[...] = jnp.zeros(vscr.shape, F32)
-    nown = vscr.shape[0]
 
     def vec(r, value):
         n = widths[r]
-        pick, mine = spread(n * nown, n, nown)
+        pick, mine = made[n]
         vscr[:, r, 0:LANE] = lax.dot_general(value * mine, pick, (((1,), (1,)), ((), ())), precision=lax.Precision.HIGHEST, preferred_element_type=F32)
 
-    gload.wait()
-    loads[0].wait()
-    half = 512
-
-    def feed(at):
+    post, (st0, st1, st2, st3), (t0, t1, t2), done = scatter_tasks(gs, pieces, tpart, shares, tgrad, hold, sems)
+    D0, D1, U0, U1, OUT, KV, QQ, VEC = range(8)
+    step = dstage.shape[1]
+
+    def drain(slot):
+        pltpu.make_async_copy(dstage.at[slot], gs[0].at[pl.ds(0, step)], dsem.at[slot]).wait()
+
+    def gdown_part(i, _):
+        slot = lax.rem(i, 2)
+
+        @pl.when(i >= 2)
+        def _():
+            drain(slot)
+
+        at = pl.ds(pl.multiple_of(i * step, step), step)
+        dstage[slot] = tn(act[:, at], dres2[...].astype(BF16)).astype(BF16)
+        pltpu.make_async_copy(dstage.at[slot], gs[0].at[at], dsem.at[slot]).start()
+        return 0
+
+    lax.fori_loop(0, ff // step, gdown_part, 0)
+    drain(0)
+    drain(1)
+    post(D0)
+    post(D1)
+
+    def put(i, src, dst):
+        cp = pltpu.make_async_copy(src, dst, psem.at[i])
+        cp.start()
+        return cp
+
+    def feed_back(at):
         d = nt(dres2[...].astype(BF16), wdown[at, :])
         dpre[:, at] = (d * dpre[:, at].astype(F32)).astype(BF16)
 
-    chunks(ff, half, feed)
-
-    def gdown(at):
-        wdown[at, :] = tn(act[:, at], dres2[...].astype(BF16)).astype(BF16)
-
-    chunks(ff, half, gdown)
-    put(0)
-    loads[1].wait()
+    chunks(ff, 512, feed_back)
 
     def dmix(at):
         base[:, at] = dres2[:, at] + nt(dpre[...], wup[at, :])
 
     chunks(width, 256, dmix)
-    post(0)
-
-    def gup(at):
+    st0(D0)
+
+    def gup_part(at):
         wup[:, at] = tn(inner[...], dpre[:, at]).astype(BF16)
 
-    chunks(ff, half, gup)
-    put(1)
+    chunks(ff, 512, gup_part)
+    cp = put(0, wup, gs[1])
+    st0(D1)
     dm, normed = base[...], normed1[...]
     vec(2, jnp.sum(dm * normed, axis=0, keepdims=True))
     vec(3, jnp.sum(dm, axis=0, keepdims=True))
@@ -908,25 +887,27 @@
     d1 = inv1[:, 0:1] * (scaled - jnp.mean(scaled, axis=1, keepdims=True) - normed * jnp.mean(scaled * normed, axis=1, keepdims=True))
     base[...] = d1
     vec(1, jnp.sum(d1.astype(BF16).astype(F32), axis=0, keepdims=True))
-    post(1)
-    st0(0)
-    loads[2].wait()
+    cp.wait()
+    post(U0)
+    post(U1)
+    st1(D0)
 
     def back_out(at):
         datt[:, at] = nt(base[...].astype(BF16), wout[at, :]).astype(BF16)
 
     chunks(width, 384, back_out)
 
-    def gout(at):
+    def gout_part(at):
         wout[:, at] = tn(att[...], base[:, at].astype(BF16)).astype(BF16)
 
-    chunks(width, 384, gout)
-    put(2)
-    pumps = [lambda: st0(1), lambda: (post(2), st1(0)), lambda: (st0(2), st1(1), st2(0)), lambda: (st1(2), st2(1))]
+    chunks(width, 384, gout_part)
+    cp = put(1, wout, gs[2])
+    st0(U0)
+    pumps = [[(cp.wait,), (post, OUT), (st1, D1), (st2, D0)], [(st0, U1), (st1, U0)], [(st0, OUT), (st2, D1), (st2, U0)], [(st1, U1), (st1, OUT)]]
     for m in range(micro):
         mrow = slice(m * nrow, (m + 1) * nrow)
 
-        def attend(p, _):
+        def attend_back(p, _):
             at = pl.ds(pl.multiple_of(p * LANE, LANE), LANE)
             vat = pl.ds(pl.multiple_of(width + p * LANE, LANE), LANE)
             q2 = split_heads(qs[mrow, at].astype(F32) * head_scale)
@@ -936,15 +917,16 @@
             dprob = nt(o2, kv[m, :, vat])
             delta = jnp.sum(prob * dprob, axis=1, keepdims=True)
             ds = (prob * (dprob - delta)).astype(BF16)
-            dq[mrow, at] = (join_heads(jnp.dot(ds, kv[m, :, at], preferred_element_type=F32)) * head_scale).astype(BF16)
-            dkv[m, :, at] = tn(ds, q2).astype(BF16)
-            dkv[m, :, vat] = tn(low, o2).astype(BF16)
+            datt[mrow, at] = (join_heads(jnp.dot(ds, kv[m, :, at], preferred_element_type=F32)) * head_scale).astype(BF16)
+            kv[m, :, at] = tn(ds, q2).astype(BF16)
+            kv[m, :, vat] = tn(low, o2).astype(BF16)
             return 0
 
         for part in range(2):
-            lax.fori_loop(part * pairs // 2, (part + 1) * pairs // 2, attend, 0)
-            pumps[2 * m + part]()
-    loads[3].wait()
+            lax.fori_loop(part * pairs // 2, (part + 1) * pairs // 2, attend_back, 0)
+            for f, *a in pumps[2 * m + part]:
+                f(*a)
+    dq, dkv = datt, kv
     for m in range(micro):
 
         def piece(i, _):
@@ -955,87 +937,125 @@
 
         lax.fori_loop(0, width // 256, piece, 0)
     t0()
-
-    def dsrc(at):
-        base[:, at] = base[:, at] + nt(dq[...], wqkv[at, 0:width])
-
-    chunks(width, 256, dsrc)
-    st2(2)
-    src = tok.at[seq // XS, seq % XS]
-
-    def gq(at):
-        wqkv[:, at] = tn(src[...].reshape(count, width), dq[:, at]).astype(BF16)
-
-    chunks(width, 384, gq)
+    st2(U1)
 
     def gkv(i, _):
         at = pl.ds(pl.multiple_of(i * 384, 128), 384)
         to = pl.ds(pl.multiple_of(width + i * 384, 128), 384)
-        total = tn(tok[:, :, 0].reshape(length, width), dkv[0, :, at])
+        total = tn(tout[:, :, 0].reshape(length, width), dkv[0, :, at])
         for m in range(1, micro):
-            total = total + tn(tok[:, :, m].reshape(length, width), dkv[m, :, at])
+            total = total + tn(tout[:, :, m].reshape(length, width), dkv[m, :, at])
         wqkv[:, to] = total.astype(BF16)
         return 0
 
     lax.fori_loop(0, 2 * width // 384, gkv, 0)
-    put(3)
+    cp = put(2, wqkv.at[:, pl.ds(width, 2 * width)], gs[3].at[:, pl.ds(width, 2 * width)])
+    st2(OUT)
+    cp.wait()
+    post(KV)
+
+    def dsrc(at):
+        base[:, at] = base[:, at] + nt(dq[...], wqkv[at, 0:width])
+
+    chunks(width, 256, dsrc)
+
+    def gq(at):
+        wqkv[:, at] = tn(tok[...].reshape(count, width), dq[:, at]).astype(BF16)
+
+    chunks(width, 384, gq)
+    cp = put(3, wqkv.at[:, pl.ds(0, width)], gs[3].at[:, pl.ds(0, width)])
     dv = sum(jnp.sum(dkv[m, :, width:].astype(F32), axis=0, keepdims=True) for m in range(micro))
     vec(0, jnp.concatenate([jnp.sum(dq[...].astype(F32), axis=0, keepdims=True), dv], axis=1))
     vec(4, jnp.sum(dpre[...].astype(F32), axis=0, keepdims=True))
-    post(3)
     for r in range(3):
         vec(5 + r, sums[r : r + 1])
-    put(4)
-    st3(0)
-    post(4)
-    st0(3)
+    cp.wait()
+    post(QQ)
+    st0(KV)
+    cp = put(4, vscr, gs[4].reshape(vscr.shape))
     t1()
-    st3(1)
-    st0(4)
-    st3(2)
-    st1(3)
-    st1(4)
+    cp.wait()
+    post(VEC)
+    st0(QQ)
+    st0(VEC)
+    for w in (D0, D1, U0, U1):
+        st3(w)
+    st1(KV)
+    st1(QQ)
+    st1(VEC)
     t2()
-    st2(3)
-    st2(4)
-    st3(3)
-    st3(4)
+    st3(OUT)
+    for w in (KV, QQ, VEC):
+        st2(w)
+    for w in (KV, QQ, VEC):
+        st3(w)
     done()
-
-
-def back(weights, saved, widths):
+    run("end")
+
+
+def mega(small, shards, tok, cot, starts):
     D, V, ANY = pltpu.SemaphoreType.DMA, pltpu.VMEM, pl.ANY
+    micro, nrow, width = tok.shape
+    count, length, ff = micro * nrow, nrow * YS * XS, shards[2].shape[1]
+    pairs = micro * width // LANE
     S = jax.ShapeDtypeStruct
-    tok = saved[0]
+    widths = tuple(v.shape[1] for v in small)
     total = ZS * CS * YS * XS
-    micro, nrow, width = tok.shape[2:]
-    count, length = micro * nrow, nrow * YS * XS
-    ff = saved[8].shape[1]
-    blocks = [(w.shape[0] // total, w.shape[1]) for w in weights] + [(8, 256)]
-    kinds = [BF16] * 4 + [F32]
-    both = list(zip(blocks, kinds))
-    outs = [S(b, F32) for b in blocks] + [S((micro, nrow, width), F32)]
-    outs += [S((total * b[0], b[1]), t) for b, t in both]
-    scr = [V((total * b[0], b[1]), BF16) for b in blocks[:4]]
-    scr += [V((count, ff), BF16), V((micro, length, 2 * width), BF16), V((count, width), BF16), V((count, width), BF16)]
-    scr += [V(tok.shape, BF16), V((total, 8, 256), F32)]
+    vshape = (8, 256)
+    order = (3, 2, 1, 0)
+    garr = [(shards[i].shape, BF16) for i in order] + [(vshape, F32)]
+    pieces = ((0, 0, width // 3), (0, width // 3, width - width // 3), (1, 0, ff // 2), (1, ff // 2, ff // 2), (2, 0, width), (3, width, 2 * width), (3, 0, width), (4, 0, 256))
+    outs = [S((total * vshape[0], vshape[1]), F32)] + [S((total * s.shape[0], s.shape[1]), BF16) for s in shards]
+    outs += [S((total * b[0], b[1]), t) for b, t in garr]
+    res = [S((count, width), BF16)] + [S(b, F32) for b, _ in garr] + [S((micro, nrow, width), F32)]
+    scr = [
+        V(vshape, F32), V((YS, XS) + tok.shape, BF16), V((pairs, 2 * nrow, length), BF16), V((count, width), BF16),
+        V((micro, length, 2 * width), BF16), V((count, width), BF16), V((count, width), F32), V((count, LANE), F32),
+        V((count, width), BF16), V((count, ff), BF16), V((count, ff), BF16), V((count, width), F32), V((8, ff), F32), V((8, width), F32),
+    ]
+    scr += [V((total * s.shape[0], s.shape[1]), BF16) for s in shards]
+    scr += [V((total,) + vshape, F32), V((micro, nrow, length), F32), V((count, width), BF16), V((2, 512, width), BF16)]
+    both = [((garr[a][0][0], m), garr[a][1]) for a, _, m in pieces]
     scr += [V((ZS, YS, XS) + b, t) for b, t in both] * 2
     scr += [V((ZS, 2, b[0], b[1] // 2), t) for b, t in both] * 2
     scr += [V((ZS, b[0], b[1] // 2), t) for b, t in both] * 2
     scr += [V((ZS - 1,) + b, t) for b, t in both]
     th = (micro, nrow, width // 2)
     scr += [V((2,) + th, BF16)] * 2 + [V(th, BF16)] * 2 + [V((count, width), F32)]
-    scr += [D((4,)), D((1,)), D((5, 16)), D((5,)), D((5, 8)), D((5, 8)), D((4,)), D((4,)), D((5, 16)), D((5, 16))]
+    n, q = 5, len(pieces)
+    scr += [D((n,)), D((n,)), D((2,))]
+    scr += [D((n + 1,)), D((n, 3)), D((n, 3))] + [D((n, 4))] * 8 + [D((n, 4, 4))] * 2 + [D((4,))] * 2
+    scr += [D((q, 16)), D((q, 8)), D((q, 8)), D((4,)), D((4,)), D((q, 16)), D((q, 16))]
     spec = lambda s: pl.BlockSpec(memory_space=s)
+    got = pl.pallas_call(
+        functools.partial(mega_body, widths, pieces),
+        out_shape=outs + res,
+        in_specs=[spec(V)] * (len(small) + 6) + [spec(pltpu.SMEM)],
+        out_specs=[spec(ANY)] * 10 + [spec(V)] * len(res),
+        scratch_shapes=scr,
+        compiler_params=pltpu.CompilerParams(collective_id=0, has_side_effects=True, vmem_limit_bytes=67043328),
+        name="layer",
+    )(*small, *shards, tok, cot, starts)
+    return got[10:]
+
+
+def finish_body(widths, *refs):
+    n = 6
+    ins, vec, outs, small = refs[:n], refs[n], refs[n + 1 : 2 * n + 1], refs[2 * n + 1 :]
+    for a, b in zip(ins, outs):
+        b[...] = a[...]
+    for r, o in enumerate(small):
+        o[...] = vec[r : r + 1, 0 : widths[r]]
+
+
+def finish(arrays, vec, widths):
+    S = jax.ShapeDtypeStruct
+    outs = [S(a.shape, a.dtype) for a in arrays] + [S((1, w), F32) for w in widths]
+    spec = pl.BlockSpec(memory_space=pltpu.VMEM)
     return pl.pallas_call(
-        functools.partial(back_body, widths),
-        out_shape=outs,
-        in_specs=[spec(ANY)] * 4 + [spec(V)] * 9 + [spec(ANY)] + [spec(V)] * 3,
-        out_specs=[spec(V)] * 6 + [spec(ANY)] * 5,
-        scratch_shapes=scr,
-        compiler_params=pltpu.CompilerParams(collective_id=1, has_side_effects=True, vmem_limit_bytes=67043328),
-        name="back",
-    )(*weights, *saved)
+        functools.partial(finish_body, widths), out_shape=outs,
+        in_specs=[spec] * (len(arrays) + 1), out_specs=[spec] * len(outs), name="finish",
+    )(*arrays, vec)
 
 
 def fits(mesh):
@@ -1049,18 +1069,16 @@
     micro, _, nrow, width = tokens.shape
     small = (qv_bias, out_bias, norm1_gain, norm1_bias, up_bias, down_bias, norm2_gain, norm2_bias)
     widths = tuple(v.shape[0] for v in small)
-    vector = jnp.stack([jnp.pad(v.astype(F32), (0, 256 - v.shape[0])) for v in small])
-    cot = grad_out.reshape(micro * nrow, width)
-    got = front(
-        (vector, qkv_weight, out_weight, up_weight, down_weight), tokens[:, 0], cot, piece_starts[:, 0], widths
+    got = mega(
+        tuple(v.reshape(1, -1) for v in small), (qkv_weight, out_weight, up_weight, down_weight),
+        tokens[:, 0], grad_out.reshape(micro * nrow, width), piece_starts[:, 0],
     )
-    gqkv, gout, gup, gdown = got[1:5]
-    layer_out = got[6]
-    shares = back((gdown, gup, gout, gqkv), (got[5],) + tuple(got[7:]), widths)
-    down, up, out, qkv, vec, tokens_grad = shares[:6]
-    v = [vec[r, :n] for r, n in enumerate(widths)]
+    lout, down, up, out, qkv, vec, tgrad = got
+    done = finish((lout, tgrad, qkv, out, up, down), vec, widths)
+    lout, tgrad, qkv, out, up, down = done[:6]
+    v = [a.reshape(-1) for a in done[6:]]
     return (
-        layer_out.reshape(tokens.shape), tokens_grad.reshape(tokens.shape),
+        lout.reshape(tokens.shape), tgrad.reshape(tokens.shape),
         qkv, v[0], out, v[1], v[2], v[3], up, v[4], down, v[5], v[6], v[7],
     )
 

time: 237 us -> 196 us (0.83)
  Pallas kernels: 218 us -> 195 us
  local copies, waits for them, and re-layouts: 17.7 us -> 0 us
    pallas_call x2, Pallas kernels: 218 us -> 195 us  [the longest x1 192 us: mega(): pl.pallas_call(functools.partial(mega_body, widths, pieces), out_shape=ou...]
    unnamed x10 -> x0, local copies, waits for them, and re-layouts: 8.42 us -> none
    pad x8 -> x0, local copies, waits for them, and re-layouts: 5.28 us -> none  [fast_device(): jnp.pad(v.astype(F32), (0, 256 - v.shape[0]))]
    squeeze x3 -> x0, local copies, waits for them, and re-layouts: 3.88 us -> none  [fast_device(): v = [vec[r, :n] for r, n in enumerate(widths)]]
where the time goes in v3:
time: 196 us
  Pallas kernels  195 us (99%)
    pallas_call x1, Pallas kernels, mega(): pl.pallas_call(functools.partial(mega_body, widths, pieces), out_shape=ou...  192 us

profile of v3, /device:TPU:0, one launch (start us, length us, event | category | flops | bytes accessed | tf_op | source)
XLA Modules:
  0.0 195.7 jit_solution(194998525791621626)
XLA Ops:
  0.7 192.0 %layer.1 = (f32[256,256]{1,0:T(8,128)}, bf16[768,2304]{1,0:T(8,128)(2,1)}, bf16[768,768]{1,0:T(8,128)(2,1)}, bf16[768,3072]{1,0:T(8,128)(2,1)}, bf16[3072,768]{1...) custom-call(bf16[1,48]{1,0:T(2,128)(2,1)} %bitcast.28, ...), custom_call_target="tpu_custom_call" | custom-call | tf_op jit(solution)/shard_map/layer/pallas_call | solution.py:1030
  192.6 2.9 %finish.1 = (bf16[256,768]{1,0:T(8,128)(2,1)}, f32[2,128,768]{2,1,0:T(8,128)}, f32[24,2304]{1,0:T(8,128)}, f32[24,768]{1,0:T(8,128)}, f32[24,3072]{1,0:T(8,128)}...) custom-call(bf16[256,768]{1,0:T(8,128)(2,1)} %get-tuple-element.35.r, ...), custom_call_target="tpu_custom_call" | custom-call | tf_op jit(solution)/shard_map/finish/pallas_call | solution.py:1055

commit v4 on v3

--- a/solution.py
+++ b/solution.py
@@ -369,6 +369,8 @@
 
 MESH = pl.DeviceIdType.MESH
 ZS, CS, YS, XS = 4, 2, 2, 2
+MIDS = ()
+RMIDS = (0, 1)
 def place():
     dp = lax.axis_index("dp"); seq = lax.axis_index("seq")
     return dp // CS, dp % CS, seq // XS, seq % XS
@@ -388,7 +390,7 @@
 
 def gather_tasks(ins, tok, outs, tout, sems):
     n = len(ins)
-    (loc, zs, zr, xs, xr, ys, yr, as_, ar, bs, br, cs, cr, ts, tr) = sems
+    (loc, zs, zr, xs, xr, ys, yr, as_, ar, bs, br, cs, cr, ts, tr, es, er, us, ur, vs, vr) = sems
     z, c, y, x = place()
     X, Y = 1 - x, 1 - y
     xn, yn, cn = dev(z, c, y, X), dev(z, c, Y, x), dev(z, 1 - c, y, x)
@@ -396,13 +398,44 @@
     def rc(src, dst, s, r, d):
         return pltpu.make_async_remote_copy(src_ref=src, dst_ref=dst, send_sem=s, recv_sem=r, device_id=d, device_id_type=MESH)
 
-    sent, local = [], []
+    sent, local, maybe = [], [], []
 
     def go(cp):
         cp.start()
         sent.append(cp)
 
     hh = tok.shape[-1] // 2
+
+    def far(k):
+        return (z == 0) & (k == 3) | (z == ZS - 1) & (k == 1)
+
+    def zcast(at, s, r):
+        for k in (1, 2, 3):
+            cp = rc(at(z)[0], at(z)[1], s.at[k - 1], r.at[k - 1], dev((z + k) % ZS, c, y, x))
+            if k == 2:
+                go(cp)
+                continue
+            there = jnp.logical_not(far(k))
+            pl.when(there)(cp.start)
+            maybe.append((there, cp))
+
+    def zpass(at, s, r):
+        inner = (z == 1) | (z == 2)
+        b = at(jnp.where(z == 2, 0, ZS - 1))[1]
+        cp = rc(b, b, s.at[3], r.at[jnp.where(z == 2, 2, 0)], dev(jnp.where(z == 2, ZS - 1, 0), c, y, x))
+        pl.when(inner)(cp.start)
+        maybe.append((inner, cp))
+
+    def own_at(w):
+        return lambda q: (ins[w] if q is z else None, block(outs[w], ins[w].shape[0], q, c, y, x))
+
+    def a_at(w):
+        h = ins[w].shape[-1] // 2
+        return lambda q: (block(outs[w], ins[w].shape[0], q, c, y, X, pl.ds(0, h)),) * 2
+
+    def b_at(w):
+        h = ins[w].shape[-1] // 2
+        return lambda q: (block(outs[w], ins[w].shape[0], q, c, Y, x, pl.ds(h, h)),) * 2
 
     def begin():
         greet(z, c, y, x)
@@ -413,35 +446,77 @@
             local.append(cp)
         for w in range(n):
             o = block(outs[w], ins[w].shape[0], z, c, y, x)
-            for k in (1, 2, 3):
-                go(rc(ins[w], o, zs.at[w, k - 1], zr.at[w, k - 1], dev((z + k) % ZS, c, y, x)))
             go(rc(ins[w], o, xs.at[w, 0], xr.at[w, 0], xn))
             go(rc(ins[w], o, ys.at[w, 0], yr.at[w, 0], yn))
             go(rc(ins[w], o, cs.at[w, 0, 0], cr.at[w, 0, 0], cn))
+            cast(w)
             if w == 1:
                 to = tout.at[y, x]
                 go(rc(tok, to, ts.at[0], tr.at[0], xn))
                 go(rc(tok, to, ts.at[1], tr.at[1], yn))
 
+    def cast(w):
+        zcast(own_at(w), zs.at[w], zr.at[w])
+
     def line(w, k):
-        o = block(outs[w], ins[w].shape[0], (z + ZS - k) % ZS, c, y, x)
+        q = (z + ZS - k) % ZS
+        h = ins[w].shape[-1] // 2
+        r = ins[w].shape[0]
+        o = block(outs[w], r, q, c, y, x)
         rc(o, o, zs.at[w, k - 1], zr.at[w, k - 1], xn).wait_recv()
-        go(rc(o, o, xs.at[w, k], xr.at[w, k], xn))
-        go(rc(o, o, ys.at[w, k], yr.at[w, k], yn))
+        if k == 2:
+            zpass(own_at(w), zs.at[w], zr.at[w])
+        a, b = block(outs[w], r, q, c, y, x, pl.ds(0, h)), block(outs[w], r, q, c, y, x, pl.ds(h, h))
+        go(rc(b if w in MIDS else o, b if w in MIDS else o, xs.at[w, k], xr.at[w, k], xn))
+        go(rc(a if w in MIDS else o, a if w in MIDS else o, ys.at[w, k], yr.at[w, k], yn))
         go(rc(o, o, cs.at[w, k, 0], cr.at[w, k, 0], cn))
 
-    def relay(w, k):
+    def sides(w, k):
+        if w not in MIDS:
+            return
         q = (z + ZS - k) % ZS
-        bx, by = block(outs[w], ins[w].shape[0], q, c, y, X), block(outs[w], ins[w].shape[0], q, c, Y, x)
+        a, b = a_at(w)(q)[0], b_at(w)(q)[0]
+        rc(a, a, us.at[w, k - 1], ur.at[w, k - 1], xn).wait_recv()
+        if k == 2:
+            zpass(a_at(w), us.at[w], ur.at[w])
+        go(rc(a, a, as_.at[w, k], ar.at[w, k], yn))
+        rc(b, b, vs.at[w, k - 1], vr.at[w, k - 1], xn).wait_recv()
+        if k == 2:
+            zpass(b_at(w), vs.at[w], vr.at[w])
+        go(rc(b, b, bs.at[w, k], br.at[w, k], xn))
+
+    def pairs(w, k):
+        q = (z + ZS - k) % ZS
         h = ins[w].shape[-1] // 2
-        rc(bx, bx, xs.at[w, k], xr.at[w, k], xn).wait_recv()
-        a = block(outs[w], ins[w].shape[0], q, c, y, X, pl.ds(0, h))
-        go(rc(a, a, as_.at[w, k], ar.at[w, k], yn))
+        r = ins[w].shape[0]
+        bx, by = block(outs[w], r, q, c, y, X), block(outs[w], r, q, c, Y, x)
+        b, a = block(outs[w], r, q, c, y, X, pl.ds(h, h)), block(outs[w], r, q, c, Y, x, pl.ds(0, h))
+        got = (b, a) if w in MIDS else (bx, by)
+        rc(got[0], got[0], xs.at[w, k], xr.at[w, k], xn).wait_recv()
+        if w not in MIDS:
+            near = a_at(w)(q)[0]
+            go(rc(near, near, as_.at[w, k], ar.at[w, k], yn))
         go(rc(bx, bx, cs.at[w, k, 1], cr.at[w, k, 1], cn))
-        rc(by, by, ys.at[w, k], yr.at[w, k], yn).wait_recv()
-        b = block(outs[w], ins[w].shape[0], q, c, Y, x, pl.ds(h, h))
-        go(rc(b, b, bs.at[w, k], br.at[w, k], xn))
+        rc(got[1], got[1], ys.at[w, k], yr.at[w, k], yn).wait_recv()
+        if w not in MIDS:
+            near = b_at(w)(q)[0]
+            go(rc(near, near, bs.at[w, k], br.at[w, k], xn))
         go(rc(by, by, cs.at[w, k, 2], cr.at[w, k, 2], cn))
+
+    def relay(w):
+        bx, by = block(outs[w], ins[w].shape[0], z, c, y, X), block(outs[w], ins[w].shape[0], z, c, Y, x)
+        rc(bx, bx, xs.at[w, 0], xr.at[w, 0], xn).wait_recv()
+        a = a_at(w)(z)[0]
+        go(rc(a, a, as_.at[w, 0], ar.at[w, 0], yn))
+        if w in MIDS:
+            zcast(a_at(w), us.at[w], ur.at[w])
+        go(rc(bx, bx, cs.at[w, 0, 1], cr.at[w, 0, 1], cn))
+        rc(by, by, ys.at[w, 0], yr.at[w, 0], yn).wait_recv()
+        b = b_at(w)(z)[0]
+        go(rc(b, b, bs.at[w, 0], br.at[w, 0], xn))
+        if w in MIDS:
+            zcast(b_at(w), vs.at[w], vr.at[w])
+        go(rc(by, by, cs.at[w, 0, 2], cr.at[w, 0, 2], cn))
 
     def corner(w, k):
         h = ins[w].shape[-1] // 2
@@ -481,26 +556,34 @@
     def finish():
         for cp in sent:
             cp.wait_send()
+        for there, cp in maybe:
+            pl.when(there)(cp.wait_send)
 
     P = functools.partial
     tasks = {"start": [begin], "end": [finish]}
     K = range(ZS)
 
-    def lines(w): return [P(line, w, k) for k in K if k]
-    def relays(w): return [P(relay, w, k) for k in K]
-    def ends(w): return [P(corner, w, k) for k in K]
-    def last(w): return [P(arrive, w, k) for k in K] + [P(own, w)]
-
-    tasks[0] = lines(0) + lines(1) + relays(0) + relays(1) + [tok_relay] + lines(2) + lines(3) + ends(0) + ends(1)
-    tasks[1] = lines(4) + relays(2) + last(0) + last(1)
-    tasks[(2, 0)] = [tok_corner] + relays(3)[:2]
-    tasks[(2, 1)] = relays(3)[2:] + ends(2)
-    tasks[(2, 2)] = relays(4)[:1] + last(2)
-    tasks[(3, 0)] = relays(4)[1:2] + ends(3)[:1]
-    tasks[(3, 1)] = relays(4)[2:3] + ends(3)[1:2]
-    tasks[(3, 2)] = relays(4)[3:] + ends(3)[2:]
-    tasks[(3, 3)] = ends(4)[:2] + last(3)
-    tasks[4] = ends(4)[2:] + last(4)
+    ks = (2, 1, 3)
+
+    def mid(w): return [P(f, w, k) for k in ks for f in (line, sides)]
+    def meet(w): return [P(pairs, w, k) for k in ks]
+    def ends(w): return [P(corner, w, k) for k in (0,) + ks]
+    def last(w): return [P(arrive, w, k) for k in (0,) + ks] + [P(own, w)]
+
+    tasks[0] = [P(relay, 0), P(relay, 1), P(relay, 2), tok_relay, P(relay, 3), P(relay, 4)] + mid(0) + mid(1) + mid(2)
+    m3, m4, e3 = mid(3), mid(4), meet(3)
+    tasks[1] = m3 + meet(0) + meet(1) + m4[:4] + meet(2) + ends(0) + ends(1) + m4[4:] + last(0) + last(1)
+    tasks[(2, 0)] = [tok_corner] + e3[:1]
+    tasks[(2, 1)] = e3[1:] + ends(2)
+    tasks[(2, 2)] = meet(4)[:1] + last(2)
+    tasks[(3, 0)] = meet(4)[1:2] + ends(3)[:2]
+    tasks[(3, 1)] = meet(4)[2:]
+    tasks[(3, 2)] = ends(3)[2:]
+    e4 = ends(4)
+    tasks[(3, 3)] = last(3) + e4[:1]
+    for part in range(3):
+        tasks[(4, part)] = [e4[part + 1]]
+    tasks[4] = last(4)
     return tasks
 
 
@@ -582,6 +665,20 @@
     def s2b(w): return rc(hs[w].at[:, y, X, :, B[w]], r2bs[w], ss.at[w, 4], sr.at[w, 4], xn)
     def s3(w, k): return rc(hs[w].at[(z + k) % ZS, y, x], rzs[w].at[k - 1], ss.at[w, 4 + k], sr.at[w, 4 + k], dev((z + k) % ZS, c, y, x))
 
+    def m1a(w): return rc(hs[w].at[:, Y, :, :, A[w]], ras[w], ss.at[w, 1], sr.at[w, 1], yn)
+    def m1b(w): return rc(hs[w].at[:, :, X, :, B[w]], rys[w], ss.at[w, 2], sr.at[w, 2], xn)
+
+    def m2a(w, k):
+        q = (z + k) % ZS
+        return rc(hs[w].at[q, y, :, :, A[w]], r2as[w].at[k - 1], ss.at[w, 2 + k], sr.at[w, 2 + k], dev(q, c, y, x))
+
+    def m2b(w, k):
+        q = (z + k) % ZS
+        return rc(hs[w].at[q, :, x, :, B[w]], r2bs[w].at[k - 1], ss.at[w, 5 + k], sr.at[w, 5 + k], dev(q, c, y, x))
+
+    def m3a(w): return rc(hs[w].at[z, y, X, :, A[w]], rzs[w].at[0], ss.at[w, 9], sr.at[w, 9], xn)
+    def m3b(w): return rc(hs[w].at[z, Y, x, :, B[w]], rzs[w].at[1], ss.at[w, 10], sr.at[w, 10], yn)
+
     def post(w):
         for k in range(len(spots)):
             load(w, k).start()
@@ -602,10 +699,49 @@
             return 0
 
         lax.fori_loop(0, ZS, one, 0)
-        go(s1a(w))
-        go(s1b(w))
+        go(m1a(w) if w in RMIDS else s1a(w))
+        go(m1b(w) if w in RMIDS else s1b(w))
+
+    def mid1(w):
+        m1a(w).wait_recv()
+        m1b(w).wait_recv()
+
+        def one(i, _):
+            for j in range(2):
+                hs[w][i, y, j, :, A[w]] = plus(hs[w][i, y, j, :, A[w]], ras[w][i, j], hs[w].dtype)
+                hs[w][i, j, x, :, B[w]] = plus(hs[w][i, j, x, :, B[w]], rys[w][i, j], hs[w].dtype)
+            return 0
+
+        lax.fori_loop(0, ZS, one, 0)
+        for k in (2, 1, 3):
+            go(m2a(w, k))
+            go(m2b(w, k))
+
+    def mid2(w):
+        for k in (1, 2, 3):
+            m2a(w, k).wait_recv()
+            m2b(w, k).wait_recv()
+        for j in range(2):
+            a, b = hs[w][z, y, j, :, A[w]].astype(F32), hs[w][z, j, x, :, B[w]].astype(F32)
+            for k in range(ZS - 1):
+                a = a + r2as[w][k, j].astype(F32)
+                b = b + r2bs[w][k, j].astype(F32)
+            hs[w][z, y, j, :, A[w]] = a.astype(hs[w].dtype)
+            hs[w][z, j, x, :, B[w]] = b.astype(hs[w].dtype)
+        go(m3a(w))
+        go(m3b(w))
+
+    def mid3(w):
+        m3a(w).wait_recv()
+        m3b(w).wait_recv()
+        arr, col, size = pieces[w]
+        for i, cols in enumerate((A[w], B[w])):
+            own = hs[w][z, y, x, :, cols].astype(F32) + rzs[w][i].astype(F32)
+            outs[arr][:, pl.ds(col + i * (size // 2), size // 2)] = own
 
     def st1(w):
+        if w in RMIDS:
+            return mid1(w)
         s1a(w).wait_recv()
         s1b(w).wait_recv()
 
@@ -620,6 +756,8 @@
         go(s2b(w))
 
     def st2(w):
+        if w in RMIDS:
+            return mid2(w)
         s2a(w).wait_recv()
         s2b(w).wait_recv()
 
@@ -633,6 +771,8 @@
             go(s3(w, k))
 
     def st3(w):
+        if w in RMIDS:
+            return mid3(w)
         total = hs[w][z, y, x].astype(F32)
         for k in (1, 2, 3):
             s3(w, k).wait_recv()
@@ -684,8 +824,8 @@
     base = hold[-1]
     k += 7 * np_ + 5
     wsem, psem, dsem = refs[k : k + 3]
-    comm = refs[k + 3 : k + 18]
-    sems = refs[k + 18 :]
+    comm = refs[k + 3 : k + 24]
+    sems = refs[k + 24 :]
     gvec, gqkv, gout, gup, gdown = gweights
     mixed, gp, vscr = base, dpre, vecs
     spare = tok.shape[0] * tok.shape[1] * YS * XS
@@ -802,7 +942,9 @@
         act[:, at] = (pre * cdf).astype(BF16)
         gp[:, at] = (cdf + pre * jnp.exp(-0.5 * pre * pre) * (1.0 / math.sqrt(2.0 * math.pi))).astype(BF16)
 
-    chunks(ff, 512, feed)
+    for part in range(3):
+        lax.fori_loop(2 * part, 2 * part + 2, lambda i, _: (feed(pl.ds(pl.multiple_of(i * (ff // 6), 128), ff // 6)), 0)[1], 0)
+        run((4, part))
     run(4)
     last = fetch(4)
     last.wait()
@@ -836,25 +978,31 @@
     D0, D1, U0, U1, OUT, KV, QQ, VEC = range(8)
     step = dstage.shape[1]
 
-    def drain(slot):
-        pltpu.make_async_copy(dstage.at[slot], gs[0].at[pl.ds(0, step)], dsem.at[slot]).wait()
-
-    def gdown_part(i, _):
-        slot = lax.rem(i, 2)
-
-        @pl.when(i >= 2)
-        def _():
-            drain(slot)
-
-        at = pl.ds(pl.multiple_of(i * step, step), step)
-        dstage[slot] = tn(act[:, at], dres2[...].astype(BF16)).astype(BF16)
-        pltpu.make_async_copy(dstage.at[slot], gs[0].at[at], dsem.at[slot]).start()
-        return 0
-
-    lax.fori_loop(0, ff // step, gdown_part, 0)
-    drain(0)
-    drain(1)
+    def gdown_cols(col, size):
+        cols = pl.ds(col, size)
+
+        def send(slot, at):
+            return pltpu.make_async_copy(dstage.at[slot, :, pl.ds(0, size)], gs[0].at[at, cols], dsem.at[slot])
+
+        def one(i, _):
+            slot = lax.rem(i, 2)
+
+            @pl.when(i >= 2)
+            def _():
+                send(slot, pl.ds(0, step)).wait()
+
+            at = pl.ds(pl.multiple_of(i * step, step), step)
+            dstage[slot, :, 0:size] = tn(act[:, at], dres2[:, cols].astype(BF16)).astype(BF16)
+            send(slot, at).start()
+            return 0
+
+        lax.fori_loop(0, ff // step, one, 0)
+        send(0, pl.ds(0, step)).wait()
+        send(1, pl.ds(0, step)).wait()
+
+    gdown_cols(*pieces[D0][1:])
     post(D0)
+    gdown_cols(*pieces[D1][1:])
     post(D1)
 
     def put(i, src, dst):
@@ -866,20 +1014,21 @@
         d = nt(dres2[...].astype(BF16), wdown[at, :])
         dpre[:, at] = (d * dpre[:, at].astype(F32)).astype(BF16)
 
+    st0(D0)
     chunks(ff, 512, feed_back)
+    st0(D1)
 
     def dmix(at):
         base[:, at] = dres2[:, at] + nt(dpre[...], wup[at, :])
 
     chunks(width, 256, dmix)
-    st0(D0)
+    st1(D0)
 
     def gup_part(at):
         wup[:, at] = tn(inner[...], dpre[:, at]).astype(BF16)
 
     chunks(ff, 512, gup_part)
     cp = put(0, wup, gs[1])
-    st0(D1)
     dm, normed = base[...], normed1[...]
     vec(2, jnp.sum(dm * normed, axis=0, keepdims=True))
     vec(3, jnp.sum(dm, axis=0, keepdims=True))
@@ -890,7 +1039,6 @@
     cp.wait()
     post(U0)
     post(U1)
-    st1(D0)
 
     def back_out(at):
         datt[:, at] = nt(base[...].astype(BF16), wout[at, :]).astype(BF16)
@@ -902,8 +1050,9 @@
 
     chunks(width, 384, gout_part)
     cp = put(1, wout, gs[2])
+    st1(D1)
     st0(U0)
-    pumps = [[(cp.wait,), (post, OUT), (st1, D1), (st2, D0)], [(st0, U1), (st1, U0)], [(st0, OUT), (st2, D1), (st2, U0)], [(st1, U1), (st1, OUT)]]
+    pumps = [[(cp.wait,), (post, OUT), (st2, D0)], [(st0, U1), (st1, U0)], [(st0, OUT), (st2, D1), (st2, U0)], [(st1, U1), (st1, OUT)]]
     for m in range(micro):
         mrow = slice(m * nrow, (m + 1) * nrow)
 
@@ -1018,14 +1167,15 @@
     both = [((garr[a][0][0], m), garr[a][1]) for a, _, m in pieces]
     scr += [V((ZS, YS, XS) + b, t) for b, t in both] * 2
     scr += [V((ZS, 2, b[0], b[1] // 2), t) for b, t in both] * 2
-    scr += [V((ZS, b[0], b[1] // 2), t) for b, t in both] * 2
-    scr += [V((ZS - 1,) + b, t) for b, t in both]
+    scr += [V(((ZS - 1, 2) if w in RMIDS else (ZS,)) + (b[0], b[1] // 2), t) for w, (b, t) in enumerate(both)] * 2
+    scr += [V((2, b[0], b[1] // 2) if w in RMIDS else (ZS - 1,) + b, t) for w, (b, t) in enumerate(both)]
     th = (micro, nrow, width // 2)
     scr += [V((2,) + th, BF16)] * 2 + [V(th, BF16)] * 2 + [V((count, width), F32)]
     n, q = 5, len(pieces)
     scr += [D((n,)), D((n,)), D((2,))]
-    scr += [D((n + 1,)), D((n, 3)), D((n, 3))] + [D((n, 4))] * 8 + [D((n, 4, 4))] * 2 + [D((4,))] * 2
-    scr += [D((q, 16)), D((q, 8)), D((q, 8)), D((4,)), D((4,)), D((q, 16)), D((q, 16))]
+    scr += [D((n + 1,)), D((n, 4)), D((n, 3))] + [D((n, 4))] * 8 + [D((n, 4, 4))] * 2 + [D((4,))] * 2
+    scr += [D((1,))] * 2 + [D((n, 4)), D((n, 3))] * 2
+    scr += [D((q, 16)), D((q, 12)), D((q, 12)), D((4,)), D((4,)), D((q, 16)), D((q, 16))]
     spec = lambda s: pl.BlockSpec(memory_space=s)
     got = pl.pallas_call(
         functools.partial(mega_body, widths, pieces),

time: 196 us -> 193 us (0.985)
  Pallas kernels: 195 us -> 192 us
    pallas_call x1, Pallas kernels: 192 us -> 189 us  [mega(): pl.pallas_call(functools.partial(mega_body, widths, pieces), out_shape=ou...]
where the time goes in v4:
time: 193 us; the launch traced here: 192 us
  Pallas kernels  192 us (99%)
    pallas_call x1, Pallas kernels, mega(): pl.pallas_call(functools.partial(mega_body, widths, pieces), out_shape=ou...  189 us

profile of v4, /device:TPU:0, one launch (start us, length us, event | category | flops | bytes accessed | tf_op | source)
XLA Modules:
  0.0 192.4 jit_solution(16957808955259705444)
XLA Ops:
  0.7 188.7 %layer.1 = (f32[256,256]{1,0:T(8,128)}, bf16[768,2304]{1,0:T(8,128)(2,1)}, bf16[768,768]{1,0:T(8,128)(2,1)}, bf16[768,3072]{1,0:T(8,128)(2,1)}, bf16[3072,768]{1...) custom-call(bf16[1,48]{1,0:T(2,128)(2,1)} %bitcast.28, ...), custom_call_target="tpu_custom_call" | custom-call | tf_op jit(solution)/shard_map/layer/pallas_call | solution.py:1180
  189.4 2.9 %finish.1 = (bf16[256,768]{1,0:T(8,128)(2,1)}, f32[2,128,768]{2,1,0:T(8,128)}, f32[24,2304]{1,0:T(8,128)}, f32[24,768]{1,0:T(8,128)}, f32[24,3072]{1,0:T(8,128)}...) custom-call(bf16[256,768]{1,0:T(8,128)(2,1)} %get-tuple-element.35.r, ...), custom_call_target="tpu_custom_call" | custom-call | tf_op jit(solution)/shard_map/finish/pallas_call | solution.py:1205

commit v5 on v4

--- a/solution.py
+++ b/solution.py
@@ -369,8 +369,8 @@
 
 MESH = pl.DeviceIdType.MESH
 ZS, CS, YS, XS = 4, 2, 2, 2
-MIDS = ()
-RMIDS = (0, 1)
+MIDS = (2,)
+RMIDS = (0, 1, 2)
 def place():
     dp = lax.axis_index("dp"); seq = lax.axis_index("seq")
     return dp // CS, dp % CS, seq // XS, seq % XS
@@ -1050,9 +1050,7 @@
 
     chunks(width, 384, gout_part)
     cp = put(1, wout, gs[2])
-    st1(D1)
-    st0(U0)
-    pumps = [[(cp.wait,), (post, OUT), (st2, D0)], [(st0, U1), (st1, U0)], [(st0, OUT), (st2, D1), (st2, U0)], [(st1, U1), (st1, OUT)]]
+    pumps = [[(cp.wait,), (post, OUT), (st0, U0)], [(st0, U1), (st1, D1)], [(st0, OUT)], [(st1, U0)]]
     for m in range(micro):
         mrow = slice(m * nrow, (m + 1) * nrow)
 
@@ -1086,7 +1084,6 @@
 
         lax.fori_loop(0, width // 256, piece, 0)
     t0()
-    st2(U1)
 
     def gkv(i, _):
         at = pl.ds(pl.multiple_of(i * 384, 128), 384)
@@ -1099,9 +1096,9 @@
 
     lax.fori_loop(0, 2 * width // 384, gkv, 0)
     cp = put(2, wqkv.at[:, pl.ds(width, 2 * width)], gs[3].at[:, pl.ds(width, 2 * width)])
-    st2(OUT)
     cp.wait()
     post(KV)
+    st1(U1)
 
     def dsrc(at):
         base[:, at] = base[:, at] + nt(dq[...], wqkv[at, 0:width])
@@ -1122,20 +1119,24 @@
     post(QQ)
     st0(KV)
     cp = put(4, vscr, gs[4].reshape(vscr.shape))
-    t1()
+    st1(OUT)
     cp.wait()
     post(VEC)
     st0(QQ)
     st0(VEC)
-    for w in (D0, D1, U0, U1):
+    st2(D0)
+    st2(U0)
+    t1()
+    st2(D1)
+    st2(U1)
+    st2(OUT)
+    for w in (KV, QQ, VEC):
+        st1(w)
+    for w in (D0, U0, D1, U1, OUT):
         st3(w)
-    st1(KV)
-    st1(QQ)
-    st1(VEC)
-    t2()
-    st3(OUT)
     for w in (KV, QQ, VEC):
         st2(w)
+    t2()
     for w in (KV, QQ, VEC):
         st3(w)
     done()

time: 193 us -> 189 us (0.979)
  Pallas kernels: 192 us -> 188 us
    pallas_call x1, Pallas kernels: 189 us -> 185 us  [mega(): pl.pallas_call(functools.partial(mega_body, widths, pieces), out_shape=ou...]
where the time goes in v5:
time: 189 us
  Pallas kernels  188 us (99%)
    pallas_call x1, Pallas kernels, mega(): pl.pallas_call(functools.partial(mega_body, widths, pieces), out_shape=ou...  185 us

profile of v5, /device:TPU:0, one launch (start us, length us, event | category | flops | bytes accessed | tf_op | source)
XLA Modules:
  0.0 188.7 jit_solution(14295290076759012243)
XLA Ops:
  0.7 185.0 %layer.1 = (f32[256,256]{1,0:T(8,128)}, bf16[768,2304]{1,0:T(8,128)(2,1)}, bf16[768,768]{1,0:T(8,128)(2,1)}, bf16[768,3072]{1,0:T(8,128)(2,1)}, bf16[3072,768]{1...) custom-call(bf16[1,48]{1,0:T(2,128)(2,1)} %bitcast.28, ...), custom_call_target="tpu_custom_call" | custom-call | tf_op jit(solution)/shard_map/layer/pallas_call | solution.py:1181
  185.7 2.9 %finish.1 = (bf16[256,768]{1,0:T(8,128)(2,1)}, f32[2,128,768]{2,1,0:T(8,128)}, f32[24,2304]{1,0:T(8,128)}, f32[24,768]{1,0:T(8,128)}, f32[24,3072]{1,0:T(8,128)}...) custom-call(bf16[256,768]{1,0:T(8,128)(2,1)} %get-tuple-element.35.r, ...), custom_call_target="tpu_custom_call" | custom-call | tf_op jit(solution)/shard_map/finish/pallas_call | solution.py:1206
